TPU v7x, 16 devices: a 4x2x1 block of a 4x4x8 slice. The times are simulated.
16 devices in a mesh: dp: 2 (over y, z), tp: 8 (over x, core).
Axes of the slice: x: 4, y: 2, z: 1, core: 2. Of those that a mesh axis runs over, the one named last changes fastest.
The devices are a block of a 4x4x8 slice.
Arguments:
- tokens: bfloat16 [6, 4096, 3072], P('dp', 'tp'), parts along dimension 0
- cond_vec: float32 [6, 3072], P('dp'), parts along dimension 0
- txt_len: int32 [6], P('dp'), parts along dimension 0
- grid_hw: int32 [6, 2], P('dp'), parts along dimension 0
- w_mod: bfloat16 [3072, 9216], replicated
- b_mod: float32 [9216], replicated
- w_qkv: bfloat16 [3072, 3, 3072], P(None, None, 'tp')
- b_qkv: float32 [3, 3072], P(None, 'tp')
- q_gain: float32 [128], replicated
- k_gain: float32 [128], replicated
- w_mlp_in: bfloat16 [3072, 12288], P(None, 'tp')
- b_mlp_in: float32 [12288], P('tp')
- w_out_attn: bfloat16 [3072, 3072], P('tp')
- w_out_mlp: bfloat16 [12288, 3072], P('tp')
- b_out: float32 [3072], replicated
Outputs:
- output: bfloat16 [6, 4096, 3072], P('dp', 'tp'), parts along dimension 0
There are 2 independent parts. A program takes and returns all parts, laid end to end along the dimension named above; an argument that names none is the same for every part.
All inputs are finite; a program needn't handle non-finite values.
Results may differ from a plain program's by a relative error of at most 0.00358401.
Values are sent between devices in bfloat16 or wider.
A program may use at most 768 MiB of HBM per device.

v0:
```python
import jax
import jax.numpy as jnp
from jax import lax
from jax.sharding import PartitionSpec as P

HEAD = 128
TXT = 256
QBLOCK = 256
EPS = 1e-6
THETA = 256.0


def modulation(cond_vec, w_mod, b_mod):
    d_model = w_mod.shape[0]
    mod_all = jnp.dot(jax.nn.silu(cond_vec).astype(jnp.bfloat16), w_mod, preferred_element_type=jnp.float32) + b_mod
    return mod_all[:, :d_model], mod_all[:, d_model:2 * d_model], mod_all[:, 2 * d_model:]


def modulated_norm(tokens, shift, scale):
    tok_f32 = tokens.astype(jnp.float32)
    centered = tok_f32 - jnp.mean(tok_f32, axis=-1, keepdims=True)
    variance = jnp.mean(centered * centered, axis=-1, keepdims=True)
    normed = centered * lax.rsqrt(variance + EPS)
    return (normed * (1.0 + scale[:, None, :]) + shift[:, None, :]).astype(jnp.bfloat16)


def rope_table(grid_hw, seq_len):
    tok_idx = jnp.arange(seq_len, dtype=jnp.int32)[None, :]
    grid_h = grid_hw[:, 0:1]
    grid_w = grid_hw[:, 1:2]
    t_pos = tok_idx // (grid_h * grid_w)
    h_pos = (tok_idx // grid_w) % grid_h
    w_pos = tok_idx % grid_w
    pair_idx = jnp.arange(HEAD // 2, dtype=jnp.int32)
    axis_sel = (pair_idx >= 8).astype(jnp.int32) + (pair_idx >= 36).astype(jnp.int32)
    within = pair_idx - jnp.where(axis_sel == 0, 0, jnp.where(axis_sel == 1, 8, 36))
    axis_dim = jnp.where(axis_sel == 0, 16.0, 56.0)
    inv_freq = jnp.power(THETA, -2.0 * within.astype(jnp.float32) / axis_dim)
    pos_sel = jnp.where(axis_sel == 0, t_pos[..., None], jnp.where(axis_sel == 1, h_pos[..., None], w_pos[..., None]))
    angles = pos_sel.astype(jnp.float32) * inv_freq
    angles = jnp.where((tok_idx < seq_len - TXT)[..., None], angles, 0.0)
    return jnp.cos(angles), jnp.sin(angles)


def apply_rope(heads_f32, cos_t, sin_t):
    full_shape = heads_f32.shape
    pairs = heads_f32.reshape(full_shape[:-1] + (full_shape[-1] // 2, 2))
    real_part = pairs[..., 0]
    imag_part = pairs[..., 1]
    cos_b = cos_t[:, :, None, :]
    sin_b = sin_t[:, :, None, :]
    rotated = jnp.stack([real_part * cos_b - imag_part * sin_b, real_part * sin_b + imag_part * cos_b], axis=-1)
    return rotated.reshape(full_shape)


def head_rms(heads_f32, gain):
    mean_sq = jnp.mean(heads_f32 * heads_f32, axis=-1, keepdims=True)
    return heads_f32 * lax.rsqrt(mean_sq + EPS) * gain


def attention(q_heads, k_heads, v_heads, tok_valid):
    batch, seq_len, n_heads, head_dim = q_heads.shape
    qk_scale = head_dim ** -0.5
    def one_block(block_id):
        q_blk = lax.dynamic_slice_in_dim(q_heads, block_id * QBLOCK, QBLOCK, axis=1)
        q_valid = lax.dynamic_slice_in_dim(tok_valid, block_id * QBLOCK, QBLOCK, axis=1)
        same_seg = q_valid[:, :, None] == tok_valid[:, None, :]
        scores = jnp.einsum('bqhd,bkhd->bhqk', q_blk, k_heads, preferred_element_type=jnp.float32) * qk_scale
        scores = jnp.where(same_seg[:, None, :, :], scores, -1e30)
        probs = jax.nn.softmax(scores, axis=-1).astype(jnp.bfloat16)
        return jnp.einsum('bhqk,bkhd->bqhd', probs, v_heads, preferred_element_type=jnp.float32).astype(jnp.bfloat16)
    blocks = lax.map(one_block, jnp.arange(seq_len // QBLOCK))
    return jnp.moveaxis(blocks, 0, 1).reshape(batch, seq_len, n_heads, head_dim)


def branch_partial(y_mod, txt_len, grid_hw, w_qkv, b_qkv, q_gain, k_gain, w_mlp_in, b_mlp_in, w_out_attn, w_out_mlp):
    batch = y_mod.shape[0]
    seq_len = y_mod.shape[1]
    d_local = w_qkv.shape[2]
    head_shape = (batch, seq_len, d_local // HEAD, HEAD)
    qkv_f32 = jnp.einsum('bnd,dce->bnce', y_mod, w_qkv, preferred_element_type=jnp.float32) + b_qkv
    cos_t, sin_t = rope_table(grid_hw, seq_len)
    q_heads = apply_rope(head_rms(qkv_f32[:, :, 0].reshape(head_shape), q_gain), cos_t, sin_t).astype(jnp.bfloat16)
    k_heads = apply_rope(head_rms(qkv_f32[:, :, 1].reshape(head_shape), k_gain), cos_t, sin_t).astype(jnp.bfloat16)
    v_heads = qkv_f32[:, :, 2].reshape(head_shape).astype(jnp.bfloat16)
    tok_valid = jnp.arange(seq_len)[None, :] < (seq_len - TXT + txt_len)[:, None]
    attended = attention(q_heads, k_heads, v_heads, tok_valid).reshape(batch, seq_len, d_local)
    mlp_pre = jnp.einsum('bnd,df->bnf', y_mod, w_mlp_in, preferred_element_type=jnp.float32) + b_mlp_in
    mlp_act = jax.nn.gelu(mlp_pre, approximate=True).astype(jnp.bfloat16)
    attn_part = jnp.einsum('bnc,ce->bne', attended, w_out_attn, preferred_element_type=jnp.float32)
    mlp_part = jnp.einsum('bnf,fe->bne', mlp_act, w_out_mlp, preferred_element_type=jnp.float32)
    return attn_part + mlp_part


def solution(mesh):
    def local_step(tokens, cond_vec, txt_len, grid_hw, w_mod, b_mod, w_qkv, b_qkv, q_gain, k_gain, w_mlp_in, b_mlp_in, w_out_attn, w_out_mlp, b_out):
        shift, scale, gate = modulation(cond_vec, w_mod, b_mod)
        y_local = modulated_norm(tokens, shift, scale)
        y_full = lax.all_gather(y_local, 'tp', axis=1, tiled=True)
        part_sum = branch_partial(y_full, txt_len, grid_hw, w_qkv, b_qkv, q_gain, k_gain, w_mlp_in, b_mlp_in, w_out_attn, w_out_mlp)
        own_sum = lax.psum_scatter(part_sum, 'tp', scatter_dimension=1, tiled=True)
        result = tokens.astype(jnp.float32) + gate[:, None, :] * (own_sum + b_out)
        return result.astype(jnp.bfloat16)
    in_specs = (P('dp', 'tp', None), P('dp', None), P('dp'), P('dp', None), P(None, None), P(None), P(None, None, 'tp'), P(None, 'tp'), P(None), P(None), P(None, 'tp'), P('tp'), P('tp', None), P('tp', None), P(None))
    return jax.shard_map(local_step, mesh=mesh, in_specs=in_specs, out_specs=P('dp', 'tp', None), check_vma=False)
```

profile of v0, /device:TPU:112, one launch (start us, length us, event | category | flops | bytes accessed | tf_op | source)
XLA Modules:
  0.0 2597.0 jit_solution(13779713861000390209)
XLA Ops:
  15.7 20.2 convolution_add_fusion.1
  71.5 309.3 %all-gather.2.cloned.1.call-done = bf16[3,4096,3072]{2,1,0:T(8,128)(2,1)} async-done(((bf16[3,512,3072]{2,1,0:T(8,128)(2,1)}), bf16[3,4096,3072]{2,1,0:T(8,128)(2,1)}) %all-gather.2.cloned.1.call-update) | async-done | bytes 75497488 | tf_op jit(solution)/shard_map/all_gather | solution.py:99
  380.8 97.8 %fusion.34 = f32[3,4096,3,384]{1,3,2,0:T(8,128)} fusion(bf16[3,4096,3072]{2,1,0:T(8,128)(2,1)} %all-gather.2.cloned.1.call-done, f32[3,384]{1,0:T(4,128)S(1)} %copy-done.14, bf16[3072,3,384]{2,0,1:T(8,128)(2,1)} %param.25), kind=kOutput, calls=%fused_computation.34 | convolution fusion | flops 86987243520 | bytes 139203072 | tf_op jit(solution)/shard_map/bnd,dce->bnce/dot_general | solution.py:81
  488.6 36.1 %slice_multiply_fusion.1 = (f32[3,4096,1,384]{1,3,2,0:T(8,128)}, f32[3,4096,1,384]{1,3,2,0:T(8,128)}, f32[3,4096,1,384]{1,3,2,0:T(8,128)}, f32[3,4096,1,384]{1,3,2,0:T(8,128)}) fusion(f32[3,4096,3,384]{1,3,2,0:T(8,128)} %fusion.34), kind=kLoop, calls=%fused_computation.116 | loop fusion | flops 9437184 | bytes 113246208 | tf_op jit(solution)/shard_map/mul | solution.py:57
  553.8 22.4 reshape_squeeze.8
  576.2 22.5 reshape_squeeze.7
  598.7 35.3 %multiply_multiply_fusion.1 = (f32[3,4096,3,64,2]{1,4,3,2,0:T(2,128)}, f32[3,4096,3,64,2]{1,4,3,2,0:T(2,128)}) fusion(f32[3,4096,3,64,2]{1,4,3,2,0:T(2,128)} %reshape_squeeze.8, f32[64,2]{1,0:T(8,128)S(1)} %copy-done.6, f32[3,4096,3]{1,2,0:T(4,128)S(1)} %add_rsqrt_fusion, f32[64,2]{1,0:T(8,128)S(1)} %copy-done.5, f32[3,4096,3,64,2]{1,4,3,2,0:T(2,128)} %reshape_squeeze.7, ...), kind=kLoop, calls=%fused_computation.46 | loop fusion | flops 18874368 | bytes 75793408 | tf_op jit(solution)/shard_map/mul | solution.py:58
  633.9 54.6 %subtract_convert_fusion = (bf16[3,4096,3,64,1]{1,4,3,2,0:T(2,128)(2,1)}, bf16[3,4096,3,64,1]{1,4,3,2,0:T(2,128)(2,1)}, bf16[3,4096,3,64,1]{1,4,3,2,0:T(2,128)(2,1)}, bf16[3,4096,3,64,1]{1,4,3,2,0:T(2,128)(2,1)}) fusion(f32[3,4096,3,64,2]{1,4,3,2,0:T(2,128)} %get-tuple-element.102, f32[3,4096,64]{1,2,0:T(8,128)} %get-tuple-element.85, ...), kind=kLoop, calls=%fused_computation.54 | loop fusion | flops 37748736 | bytes 62914560 | tf_op jit(solution)/shard_map/convert.1
  688.6 24.1 pad_maximum_fusion.1
  739.9 24.1 pad_maximum_fusion
  778.8 715.0 %while.10 = (s32[]{:T(128)}, bf16[16,3,256,3,128]{4,2,3,1,0:T(8,128)(2,1)}, s32[16]{0:T(128)S(1)}, pred[3,4096]{1,0:T(4,128)(4,1)S(1)}, bf16[3,4096,3,128]{1,3,2...) while((s32[]{:T(128)}, ...), condition=%wide.region_7.9_spmd, body=%wide.region_4.8_spmd.sunk | while | flops 4891906048 | bytes 101876160 | solution.py:72
  783.6 21.9 fusion.102
  805.5 18.0 fusion.103
  828.3 21.9 fusion.102
  850.2 18.0 fusion.103
  873.0 21.9 fusion.102
  894.9 18.0 fusion.103
  917.6 21.9 fusion.102
  939.6 18.0 fusion.103
  962.3 21.9 fusion.102
  984.2 18.0 fusion.103
  1007.0 21.9 fusion.102
  1028.9 18.0 fusion.103
  1051.7 21.9 fusion.102
  1073.6 18.0 fusion.103
  1096.4 21.9 fusion.102
  1118.3 18.0 fusion.103
  1141.1 21.9 fusion.102
  1163.0 18.0 fusion.103
  1185.8 21.9 fusion.102
  1207.7 18.0 fusion.103
  1230.5 21.9 fusion.102
  1252.4 18.0 fusion.103
  1275.1 21.9 fusion.102
  1297.0 18.0 fusion.103
  1319.8 21.9 fusion.102
  1341.7 18.0 fusion.103
  1364.5 21.9 fusion.102
  1386.4 18.0 fusion.103
  1409.2 21.9 fusion.102
  1431.1 18.0 fusion.103
  1453.9 21.9 fusion.102
  1475.8 18.0 fusion.103
  1507.1 14.9 reshape.162
  1522.1 56.6 %fusion.50 = f32[3,4096,3072]{2,1,0:T(8,128)} fusion(bf16[3,4096,384]{1,2,0:T(8,128)(2,1)} %reshape.162, bf16[384,3072]{1,0:T(8,128)(2,1)S(1)} %copy-done), kind=kOutput, calls=%fused_computation.61 | convolution fusion | flops 28991029248 | bytes 162791424 | tf_op jit(solution)/shard_map/bnc,ce->bne/dot_general | solution.py:90
  1578.7 146.7 %fusion.31.clone.4 = bf16[3,4096,1536]{2,1,0:T(8,128)(2,1)} fusion(bf16[3,4096,3072]{2,1,0:T(8,128)(2,1)} %all-gather.2.cloned.1.call-done, f32[1536]{0:T(1024)S(1)} %copy-done.13, bf16[3072,1536]{1,0:T(8,128)(2,1)} %param.29), kind=kOutput, calls=%fused_computation.30.clone.clone.clone.1 | convolution fusion | flops 116152860672 | bytes 122689536 | tf_op jit(solution)/shard_map/bnd,df->bnf/dot_general | solution.py:88
  1725.4 133.1 %convolution_add_fusion = f32[3,4096,3072]{2,1,0:T(8,128)} fusion(f32[3,4096,3072]{2,1,0:T(8,128)} %fusion.50, bf16[1536,3072]{1,0:T(8,128)(2,1)} %param.32, bf16[3,4096,1536]{2,1,0:T(8,128)(2,1)} %fusion.31.clone.4), kind=kOutput, calls=%fused_computation.33 | convolution fusion | flops 116001865728 | bytes 349175808 | tf_op jit(solution)/shard_map/bnf,fe->bne/dot_general | solution.py:91
  1858.7 716.9 %reduce-scatter.2.cloned.1.call-done = f32[3,512,3072]{2,1,0:T(8,128)} async-done(((f32[3,4096,3072]{2,1,0:T(8,128)}), f32[3,512,3072]{2,1,0:T(8,128)}) %reduce-scatter.2.cloned.1.call-update) | async-done | bytes 18874384 | tf_op jit(solution)/shard_map/reduce_scatter | solution.py:101
  (115 shorter events, 220.1 us)
Async XLA Ops:
  6.5 1515.5 %copy-start = (bf16[384,3072]{1,0:T(8,128)(2,1)S(1)}, bf16[384,3072]{1,0:T(8,128)(2,1)}, u32[]{:S(2)}) copy-start(bf16[384,3072]{1,0:T(8,128)(2,1)} %param.31) | copy-start | bytes 7077892
  6.6 374.3 %all-gather.2.cloned.1.call-start = ((), (), s32[]{:S(2)}) async-start(), calls=%async_computation.1 | async-start | bytes 84934656 | tf_op jit(solution)/shard_map/all_gather | solution.py:99
  6.6 6.5 copy-start.2
  6.6 9.1 copy-start.7
  6.6 9.1 copy-start.8
  49.4 0.7 copy-start.11
  49.4 1.4 copy-start.12
  49.4 2.2 copy-start.15
  49.4 2.3 copy-start.10
  49.4 331.4 %copy-start.14 = (f32[3,384]{1,0:T(4,128)S(1)}, f32[3,384]{1,0:T(4,128)}, u32[]{:S(2)}) copy-start(f32[3,384]{1,0:T(4,128)} %param.26) | copy-start | bytes 13828
  49.5 2526.0 %reduce-scatter.2.cloned.1.call-start = ((), (), s32[]{:S(2)}) async-start(), calls=%async_computation.2 | async-start | bytes 169869312 | tf_op jit(solution)/shard_map/reduce_scatter | solution.py:101
  576.2 22.5 copy-start.5
  576.2 22.5 copy-start.6
  764.0 14.8 copy-start.3
  1522.1 56.6 %copy-start.13 = (f32[1536]{0:T(1024)S(1)}, f32[1536]{0:T(1024)}, u32[]{:S(2)}) copy-start(f32[1536]{0:T(1024)} %param.30) | copy-start | bytes 18436
  1858.6 716.9 %copy-start.4 = (f32[3,3072]{1,0:T(4,128)S(1)}, f32[3,3072]{1,0:T(4,128)}, u32[]{:S(2)}) copy-start(f32[3,3072]{1,0:T(4,128)} %get-tuple-element.86) | copy-start | bytes 110596
  1858.6 716.9 %copy-start.9 = (f32[3072]{0:T(1024)S(1)}, f32[3072]{0:T(1024)}, u32[]{:S(2)}) copy-start(f32[3072]{0:T(1024)} %param.33) | copy-start | bytes 36868
  2575.5 14.4 copy-start.1
Sparse Core Ops, SparseCore 0:
  49.6 331.1 all-gather.1
  1858.8 716.6 reduce-scatter.1
where the time goes:
time: 2600 us
  matrix products  1090 us (42%)
  waiting for transfers between devices  1030 us (40%)
  other arithmetic  303 us (12%)
  local copies, waits for them, and re-layouts  150 us (6%)
    reduce_scatter x1, waiting for transfers between devices, local_step(): own_sum = lax.psum_scatter(part_sum, 'tp', scatter_dimension=1, tiled=True)  717 us
    sub x16, matrix products, one_block(): probs = jax.nn.softmax(scores, axis=-1).astype(jnp.bfloat16)  350 us
    all_gather x1, waiting for transfers between devices, local_step(): y_full = lax.all_gather(y_local, 'tp', axis=1, tiled=True)  309 us
    dot_general x16, matrix products, one_block(): jnp.einsum('bhqk,bkhd->bqhd', probs, v_heads, preferred_element_type=jnp....  288 us
    dot_general x1, matrix products, branch_partial(): jnp.einsum('bnd,df->bnf', y_mod, w_mlp_in, preferred_element_type=jnp.flo...  147 us
    dot_general x1, matrix products, branch_partial(): jnp.einsum('bnf,fe->bne', mlp_act, w_out_mlp, preferred_element_type=jnp....  133 us
    dot_general x1, matrix products, branch_partial(): jnp.einsum('bnd,dce->bnce', y_mod, w_qkv, preferred_element_type=jnp.floa...  97.8 us
    eq x16, other arithmetic, one_block(): same_seg = q_valid[:, :, None] == tok_valid[:, None, :]  57.2 us
  transfers between devices with their start and end apart: 2, of which 2 were waited for; matrix products, arithmetic and copies ran while one was open for 1% of the time, Pallas kernels for 0%

commit v1 on v0

v1 whole, which is shorter than its diff:
```python
import functools
import math

import jax
import jax.numpy as jnp
from jax import lax
from jax.experimental import pallas as pl
from jax.experimental.pallas import tpu as pltpu
from jax.sharding import PartitionSpec as P


HEAD = 128
TXT = 256
EPS = 1e-6
THETA = 256.0
NT = (((1,), (1,)), ((), ()))
LOG2E = math.log2(math.e)
SCORE_EXP2 = HEAD ** -0.5 * LOG2E
VMEM = 64 * 1024 * 1024 - 128 * 1024


def qkv_kernel(y_ref, w_ref, b_ref, gain_ref, hot_ref, table_ref, q_ref, k_ref, v_ref, n_ref, *, sub):
    d_local = q_ref.shape[1]
    heads = d_local // HEAD
    stats = [None] * (3 * heads)

    def note(i, val):
        stats[i] = val if stats[i] is None else jnp.maximum(stats[i], val)

    for t in range(y_ref.shape[0] // sub):
        rows = slice(t * sub, (t + 1) * sub)
        cs = jnp.dot(hot_ref[rows, :], table_ref[...], preferred_element_type=jnp.float32)
        cs = cs[:, :2 * HEAD] + (cs[:, 2 * HEAD:4 * HEAD] + cs[:, 4 * HEAD:])
        cos_t, sin_t = cs[:, :HEAD], cs[:, HEAD:]
        hs = sub // 2
        cols = []
        for n in range(0, w_ref.shape[1], 256):
            cols.append(jnp.concatenate([jnp.dot(y_ref[t * sub + i * hs:t * sub + (i + 1) * hs, :], w_ref[:, n:n + 256], preferred_element_type=jnp.float32) for i in range(2)], axis=0))
        z = jnp.concatenate(cols, axis=1) + b_ref[...]
        for part, dst in ((0, q_ref), (1, k_ref)):
            for h in range(heads):
                x = z[:, part * d_local + h * HEAD:part * d_local + (h + 1) * HEAD]
                mean_sq = jnp.mean(x * x, axis=-1, keepdims=True)
                xn = x * lax.rsqrt(mean_sq + EPS) * gain_ref[part:part + 1, :]
                note(part * heads + h, jnp.max(jnp.sum(xn * xn, axis=-1, keepdims=True), axis=0, keepdims=True))
                rot = xn * cos_t + pltpu.roll(xn, HEAD // 2, 1) * sin_t
                dst[rows, h * HEAD:(h + 1) * HEAD] = rot.astype(jnp.bfloat16)
        v = z[:, 2 * d_local:3 * d_local]
        v_ref[rows, :] = v.astype(jnp.bfloat16)
        for h in range(heads):
            note(2 * heads + h, jnp.max(jnp.abs(v[:, h * HEAD:(h + 1) * HEAD]), axis=0, keepdims=True))
    n_ref[...] = jnp.zeros(n_ref.shape, jnp.float32)
    for i in range(3 * heads):
        n_ref[0, i:i + 1, :] = jnp.broadcast_to(stats[i], (1, HEAD))


def qkv_call(y, w, b, gains, hot, table, dl, rb=512, sub=512):
    n, d = y.shape
    d3 = w.shape[1]
    steps = n // rb
    row = lambda c: pl.BlockSpec((rb, c), lambda i: (i, 0))
    whole = lambda *s: pl.BlockSpec(s, lambda i: (0,) * len(s))
    return pl.pallas_call(
        functools.partial(qkv_kernel, sub=sub), grid=(steps,),
        in_specs=[row(d), whole(d, d3), whole(1, d3), whole(2, HEAD), row(hot.shape[1]), whole(*table.shape)],
        out_specs=[row(dl), row(dl), row(dl), pl.BlockSpec((1, 16, HEAD), lambda i: (i, 0, 0))],
        out_shape=[jax.ShapeDtypeStruct((n, dl), jnp.bfloat16)] * 3 + [jax.ShapeDtypeStruct((steps, 16, HEAD), jnp.float32)],
        compiler_params=pltpu.CompilerParams(vmem_limit_bytes=VMEM),
        cost_estimate=pl.CostEstimate(flops=2 * n * d * d3, bytes_accessed=2 * n * d + 2 * n * d3, transcendentals=0),
    )(y, w, b, gains, hot, table)


def attn_kernel(info_ref, q_ref, k_ref, v_ref, o_ref, p_ref, vx_ref, *, sub, bk):
    h = pl.program_id(0)
    i = pl.program_id(1)
    n = k_ref.shape[0]
    bq = q_ref.shape[0]
    vid = n - TXT
    n_valid = info_ref[0]
    fast = info_ref[1 + h] == 1

    def tail_rows(width):
        return lax.broadcasted_iota(jnp.int32, (TXT, width), 0) + vid

    @pl.when(i == 0)
    def _():
        vx_ref[:, :HEAD] = v_ref[...]
        vx_ref[:vid, HEAD:] = jnp.ones((vid, HEAD), jnp.bfloat16)
        keep = jnp.where(tail_rows(HEAD) < n_valid, 1.0, 0.0).astype(jnp.bfloat16)
        vx_ref[vid:, HEAD:] = keep
        vx_ref[vid:, :HEAD] = jnp.where(tail_rows(HEAD) < n_valid, v_ref[vid:, :].astype(jnp.float32), 0.0).astype(jnp.bfloat16)

    @pl.when(fast)
    def _():
        def weighted(t):
            acc = jnp.dot(p_ref[t % 2], vx_ref[...], preferred_element_type=jnp.float32)
            o_ref[t * sub:(t + 1) * sub, :] = (acc[:, :HEAD] / acc[:, HEAD:]).astype(jnp.bfloat16)

        for t in range(bq // sub):
            q = q_ref[t * sub:(t + 1) * sub, :]
            for j in range(n // bk):
                s = lax.dot_general(q, k_ref[j * bk:(j + 1) * bk, :], NT, preferred_element_type=jnp.float32)
                p_ref[t % 2, :, j * bk:(j + 1) * bk] = jnp.exp2(s * SCORE_EXP2).astype(jnp.bfloat16)
            if t > 0:
                weighted(t - 1)
        weighted(bq // sub - 1)

        @pl.when(i == n // bq - 1)
        def _():
            s = lax.dot_general(q_ref[bq - TXT:, :], k_ref[vid:, :], NT, preferred_element_type=jnp.float32)
            p = jnp.exp2(s * SCORE_EXP2).astype(jnp.bfloat16)
            pad = tail_rows(HEAD) >= n_valid
            vp = jnp.where(pad, v_ref[vid:, :].astype(jnp.float32), 0.0).astype(jnp.bfloat16)
            on = jnp.where(pad, 1.0, 0.0).astype(jnp.bfloat16)
            acc = jnp.dot(p, jnp.concatenate([vp, on], axis=1), preferred_element_type=jnp.float32)
            old = o_ref[bq - TXT:, :].astype(jnp.float32)
            o_ref[bq - TXT:, :] = jnp.where(pad, acc[:, :HEAD] / acc[:, HEAD:], old).astype(jnp.bfloat16)

    @pl.when(jnp.logical_not(fast))
    def _():
        bs = 256

        def rows(t, _):
            r0 = pl.multiple_of(t * bs, bs)
            q = q_ref[pl.ds(r0, bs), :]
            q_ok = (lax.broadcasted_iota(jnp.int32, (bs, bs), 0) + (i * bq + r0)) < n_valid

            def keys(j, carry):
                m, acc = carry
                c0 = pl.multiple_of(j * bs, bs)
                s = lax.dot_general(q, k_ref[pl.ds(c0, bs), :], NT, preferred_element_type=jnp.float32) * SCORE_EXP2
                k_ok = (lax.broadcasted_iota(jnp.int32, (bs, bs), 1) + c0) < n_valid
                s = jnp.where(q_ok == k_ok, s, -1e30)
                m_new = jnp.maximum(m, jnp.max(s, axis=1, keepdims=True))
                p = jnp.exp2(s - m_new).astype(jnp.bfloat16)
                vx = jnp.concatenate([v_ref[pl.ds(c0, bs), :], jnp.ones((bs, HEAD), jnp.bfloat16)], axis=1)
                return m_new, acc * jnp.exp2(m - m_new) + jnp.dot(p, vx, preferred_element_type=jnp.float32)

            m0 = jnp.full((bs, 1), -3e38, jnp.float32)
            _, acc = lax.fori_loop(0, n // bs, keys, (m0, jnp.zeros((bs, 2 * HEAD), jnp.float32)))
            o_ref[pl.ds(r0, bs), :] = (acc[:, :HEAD] / acc[:, HEAD:]).astype(jnp.bfloat16)
            return 0

        lax.fori_loop(0, bq // bs, rows, 0)


def attn_call(info, q, k, v, bq=1024, sub=512, bk=1024):
    n, dl = q.shape
    heads = dl // HEAD
    kv = pl.BlockSpec((n, HEAD), lambda h, i, _: (0, h))
    qo = pl.BlockSpec((bq, HEAD), lambda h, i, _: (i, h))
    return pl.pallas_call(
        functools.partial(attn_kernel, sub=sub, bk=bk),
        grid_spec=pltpu.PrefetchScalarGridSpec(
            num_scalar_prefetch=1, grid=(heads, n // bq), in_specs=[qo, kv, kv], out_specs=qo,
            scratch_shapes=[pltpu.VMEM((2, sub, n), jnp.bfloat16), pltpu.VMEM((n, 2 * HEAD), jnp.bfloat16)]),
        out_shape=jax.ShapeDtypeStruct((n, dl), jnp.bfloat16),
        compiler_params=pltpu.CompilerParams(vmem_limit_bytes=VMEM),
        cost_estimate=pl.CostEstimate(flops=8 * n * n * dl, bytes_accessed=8 * n * dl, transcendentals=n * n * heads),
    )(info, q, k, v)


def mlp_kernel(*refs, ts, steps, n_stacks, first, proj, final, aliased, nw):
    refs = list(refs)
    take = lambda k: [refs.pop(0) for _ in range(k)]
    n = len(ts)
    y_hbm = take(n if steps else 0)
    acc_hbm = take(0 if first else n)
    packs, bias = take(n_stacks), take(n_stacks)
    att_hbm = dict(zip(proj, take(len(proj))))
    oa_hbm, = take(1) if proj else (None,)
    tok_hbm, gate_ref, bout_ref = take(3) if final else (None,) * 3
    take(int(aliased))
    accs_out = [t for t in ts if t not in final]
    out_acc = dict(zip(accs_out, take(len(accs_out))))
    out_hbm, = take(1) if final else (None,)
    y_v, acc_v, w_v, u_v, h_v, bias_v, att_v, tok_v, y_sem, acc_sem, w_sem, out_sem, att_sem, tok_sem = refs
    tb, d_model = acc_v.shape[1:]
    _, _, group, width, _ = w_v.shape
    kdim = group * width
    n_steps = len(steps)
    chunk = 2 * kdim
    n_proj = d_model // chunk if proj else 0

    y_copy = lambda i: pltpu.make_async_copy(y_hbm[i], y_v.at[i], y_sem.at[i])
    acc_copy = lambda i: pltpu.make_async_copy(acc_hbm[i], acc_v.at[i], acc_sem.at[i])
    acc_store = lambda i: pltpu.make_async_copy(acc_v.at[i], out_acc[ts[i]], out_sem.at[i])
    out_rows = lambda i: pl.ds(ts[i] * tb, tb)
    tok_copy = lambda i: pltpu.make_async_copy(tok_hbm.at[out_rows(i), :], tok_v.at[final.index(ts[i])], tok_sem.at[final.index(ts[i])])
    out_store = lambda i: pltpu.make_async_copy(tok_v.at[final.index(ts[i])], out_hbm.at[out_rows(i), :], out_sem.at[i])

    def att_copies(j):
        att = att_hbm[proj[j]]
        w = att.shape[2]
        return [pltpu.make_async_copy(att.at[k], att_v.at[j, :, pl.ds(k * w, w)], att_sem.at[j, k]) for k in range(att.shape[0])]

    def weight_copies(s, slot, kind):
        if s >= n_steps:
            return [pltpu.make_async_copy(oa_hbm.at[s - n_steps, kind], w_v.at[slot, kind], w_sem.at[slot, kind, 0])]
        out, at = [], 0
        for k, (i, shard, b0, nb) in enumerate(steps[s]):
            out.append(pltpu.make_async_copy(packs[i].at[shard, kind, pl.ds(b0, nb)], w_v.at[slot, kind, pl.ds(at, nb)], w_sem.at[slot, kind, k]))
            at += nb
        return out

    def start_weights(s):
        for kind in range(2):
            for c in weight_copies(s, s % 2, kind):
                c.start()

    def arrive(s, slot):
        for kind in range(2):
            for c in weight_copies(s, slot, kind):
                c.wait()

    def follow(s, total, low):
        for k in range(low, total):
            @pl.when(s + 1 == k)
            def _():
                start_weights(k)

    def up(k, s, slot):
        t = lax.rem(k, n)
        for p in range(0, group, 2):
            w = w_v[slot, 0, p:p + 2].reshape(2 * width, d_model)
            at = slice(p * width, (p + 2) * width)
            u_v[:, at] = lax.dot_general(y_v[t], w, NT, preferred_element_type=jnp.float32) + bias_v[s, :, at]

    def act():
        h_v[...] = jax.nn.gelu(u_v[...], approximate=True).astype(jnp.bfloat16)

    def down(k, slot):
        t = lax.rem(k, n)
        for c in range(0, d_model, nw):
            w2 = w_v[slot, 1, :, :, c:c + nw].reshape(kdim, nw)
            old = acc_v[t, :, c:c + nw]
            if first:
                old = jnp.where(k < n, 0.0, old)
            acc_v[t, :, c:c + nw] = old + jnp.dot(h_v[...], w2, preferred_element_type=jnp.float32)

    total = n_steps + n_proj
    if n_steps:
        y_copy(0).start()
    start_weights(0)
    for s, parts in enumerate(steps):
        at = 0
        for i, shard, b0, nb in parts:
            for b in range(b0, b0 + nb):
                bias_v[s, :, at * width:(at + 1) * width] = bias[i][shard, b:b + 1, :]
                at += 1
    if n_steps:
        y_copy(0).wait()
        arrive(0, 0)
        for i in range(1, n):
            y_copy(i).start()
    if not first:
        for i in range(n):
            acc_copy(i).start()
    for j in range(len(proj)):
        for c in att_copies(j):
            c.start()
    for t in final:
        tok_copy(ts.index(t)).start()
    if n_steps:
        up(0, 0, 0)
        last = n * n_steps - 1

        def trip(k, _):
            s = lax.div(k, n)
            before = lax.div(k - 1, n)
            for i in range(1, n):
                @pl.when(k == i)
                def _():
                    y_copy(i).wait()
            if not first:
                for i in range(n):
                    @pl.when(k - 1 == i)
                    def _():
                        acc_copy(i).wait()
            if n_steps > 1:
                @pl.when((lax.rem(k, n) == 0) & (k > 0))
                def _():
                    arrive(0, lax.rem(s, 2))
            if total > 1:
                @pl.when(lax.rem(k, n) == 1)
                def _():
                    follow(s, total, 1)
            if not proj:
                for i in range(n - 2):
                    @pl.when(k - 2 - (last + 1 - n) == i)
                    def _():
                        acc_store(i).start()
            act()
            up(k, s, lax.rem(s, 2))
            down(k - 1, lax.rem(before, 2))
            return 0

        lax.fori_loop(1, last + 1, trip, 0)
        if not proj and n > 1:
            acc_store(n - 2).start()
        act()
        if not first and n_steps == 1:
            acc_copy(n - 1).wait()
        down(last, (n_steps - 1) % 2)
        if not proj:
            acc_store(n - 1).start()
    elif not first:
        for i in range(n):
            acc_copy(i).wait()
    if proj:
        for i, t in enumerate(ts):
            if t not in proj:
                acc_store(i).start()
        for j in range(len(proj)):
            for c in att_copies(j):
                c.wait()
        base = ts.index(proj[0])

        def turn(k, _, closing=False):
            c = lax.div(k, len(proj)) if not closing else n_proj - 1
            j = lax.rem(k, len(proj)) if not closing else k
            slot = lax.rem(n_steps + c, 2)
            if not closing:
                @pl.when(j == 0)
                def _():
                    arrive(n_steps, slot)
                    follow(n_steps + c, total, n_steps + 1)
            elif j == 0:
                arrive(n_steps, slot)
            t = proj[j] if closing else None
            last = closing and t in final
            if last:
                tok_copy(base + j).wait()
            at = c * chunk if closing else pl.multiple_of(c * chunk, chunk)
            h = att_v[j, :, pl.ds(at, chunk)]
            for e in range(0, d_model, nw):
                w2 = w_v[slot, :, :, :, e:e + nw].reshape(chunk, nw)
                part = acc_v[base + j, :, e:e + nw] + jnp.dot(h, w2, preferred_element_type=jnp.float32)
                if last:
                    f = final.index(t)
                    res = tok_v[f, :, e:e + nw].astype(jnp.float32) + gate_ref[t:t + 1, e:e + nw] * (part + bout_ref[:, e:e + nw])
                    tok_v[f, :, e:e + nw] = res.astype(jnp.bfloat16)
                else:
                    acc_v[base + j, :, e:e + nw] = part
            if closing:
                (out_store if last else acc_store)(base + j).start()
            return 0

        lax.fori_loop(0, (n_proj - 1) * len(proj), turn, 0)
        for j in range(len(proj)):
            turn(j, 0, closing=True)
    for i, t in enumerate(ts):
        (out_store if t in final else acc_store)(i).wait()


def mlp_call(ts, y, acc, stacks, steps, proj=(), att=(), w_oa=None, final=(), tail=None, group=4, nw=512):
    tb, d = (y or acc)[0].shape
    n = len(ts)
    first = acc is None
    width = 128
    hbm = pl.BlockSpec(memory_space=pl.ANY)
    vm = pl.BlockSpec(memory_space=pltpu.VMEM)
    args, specs = [], []

    def add(spec, *xs):
        args.extend(xs)
        specs.extend([spec] * len(xs))

    if steps:
        add(hbm, *y)
    if not first:
        add(hbm, *acc)
    add(hbm, *[s[0] for s in stacks])
    add(vm, *[s[1] for s in stacks])
    add(hbm, *att)
    if proj:
        add(hbm, w_oa.reshape(d // (2 * group * width), 2, group, width, d))
    alias = {}
    n_acc = n - len(final)
    outs = [jax.ShapeDtypeStruct((tb, d), jnp.float32)] * n_acc
    if final:
        tokens, gate, b_out, out = tail
        add(hbm, tokens)
        add(vm, gate, b_out)
        if out is not None:
            add(hbm, out)
            alias = {len(args) - 1: n_acc}
        outs.append(jax.ShapeDtypeStruct(tokens.shape, tokens.dtype))
    n_steps = len(steps)
    n_par = max(1, len(proj))
    has = lambda c, *s: s if c else (8, 128)
    scratch = [
        pltpu.VMEM(has(n_steps, n, tb, d), jnp.bfloat16), pltpu.VMEM((n, tb, d), jnp.float32),
        pltpu.VMEM((2, 2, group, width, d), jnp.bfloat16),
        pltpu.VMEM(has(n_steps, tb, group * width), jnp.float32), pltpu.VMEM(has(n_steps, tb, group * width), jnp.bfloat16),
        pltpu.VMEM((max(1, n_steps), 1, group * width), jnp.float32),
        pltpu.VMEM(has(proj, n_par, tb, d), jnp.bfloat16), pltpu.VMEM(has(final, max(1, len(final)), tb, d), jnp.bfloat16),
        pltpu.SemaphoreType.DMA((n,)), pltpu.SemaphoreType.DMA((n,)), pltpu.SemaphoreType.DMA((2, 2, 2)), pltpu.SemaphoreType.DMA((n,)),
        pltpu.SemaphoreType.DMA((n_par, 8)), pltpu.SemaphoreType.DMA((max(1, len(final)),))]
    cols = n_steps * group * width
    rows = n * tb
    res = pl.pallas_call(
        functools.partial(mlp_kernel, ts=tuple(ts), steps=steps, n_stacks=len(stacks), first=first, proj=tuple(proj), final=tuple(final), aliased=bool(alias), nw=nw),
        in_specs=specs, out_specs=[hbm] * len(outs), out_shape=outs, input_output_aliases=alias, scratch_shapes=scratch,
        compiler_params=pltpu.CompilerParams(vmem_limit_bytes=VMEM),
        cost_estimate=pl.CostEstimate(flops=4 * rows * d * cols + 2 * len(proj) * tb * d * d, bytes_accessed=4 * d * cols + 10 * rows * d, transcendentals=rows * cols),
    )(*args)
    return (list(res[:n_acc]), res[n_acc]) if final else (list(res), None)


def pick_kernel(where_ref, src_hbm, dst_hbm, buf, in_sem, out_sem):
    n = dst_hbm.shape[0]
    todo = [(i, j) for i in range(n) for j in range(dst_hbm.shape[1])]
    load = lambda i, j: pltpu.make_async_copy(src_hbm.at[where_ref[i], j], buf.at[i, j], in_sem.at[i, j])
    store = lambda i, j: pltpu.make_async_copy(buf.at[i, j], dst_hbm.at[i, j], out_sem.at[i, j])
    for ij in todo:
        load(*ij).start()
    for ij in todo:
        load(*ij).wait()
        store(*ij).start()
    for ij in todo:
        store(*ij).wait()


def pick_call(where, a):
    shape = (where.shape[0],) + a.shape[1:]
    hbm = pl.BlockSpec(memory_space=pl.ANY)
    return pl.pallas_call(
        pick_kernel,
        grid_spec=pltpu.PrefetchScalarGridSpec(
            num_scalar_prefetch=1, grid=(1,), in_specs=[hbm], out_specs=hbm,
            scratch_shapes=[pltpu.VMEM(shape, a.dtype), pltpu.SemaphoreType.DMA(shape[:2]), pltpu.SemaphoreType.DMA(shape[:2])]),
        out_shape=jax.ShapeDtypeStruct(shape, a.dtype),
        compiler_params=pltpu.CompilerParams(vmem_limit_bytes=VMEM),
        cost_estimate=pl.CostEstimate(flops=4 * math.prod(shape), bytes_accessed=4 * math.prod(shape), transcendentals=0),
    )(where, a)


def pack_kernel(first_ref, in_ref, out_ref, o_ref):
    o_ref[0, 0] = in_ref[...].T
    o_ref[1, 0] = out_ref[...]


def pack_call(first, count, w_in, w_out, width):
    d = w_in.shape[0]
    return pl.pallas_call(
        pack_kernel,
        grid_spec=pltpu.PrefetchScalarGridSpec(
            num_scalar_prefetch=1, grid=(count,),
            in_specs=[pl.BlockSpec((d, width), lambda i, f: (0, f[0] + i)), pl.BlockSpec((width, d), lambda i, f: (f[0] + i, 0))],
            out_specs=pl.BlockSpec((2, 1, width, d), lambda i, f: (0, i, 0, 0))),
        out_shape=jax.ShapeDtypeStruct((2, count, width, d), w_in.dtype),
        cost_estimate=pl.CostEstimate(flops=4 * count * width * d, bytes_accessed=8 * count * width * d, transcendentals=0),
    )(first[None], w_in, w_out)


def mod_kernel(me_ref, c_ref, w_ref, o_ref):
    @pl.when(pl.program_id(0) == 0)
    def _():
        o_ref[...] = jnp.zeros(o_ref.shape, jnp.float32)

    o_ref[...] += jnp.dot(c_ref[...], w_ref[...], preferred_element_type=jnp.float32)


def mod_call(me, cond, w, cols, kb=768):
    b, d = cond.shape
    return pl.pallas_call(
        mod_kernel,
        grid_spec=pltpu.PrefetchScalarGridSpec(
            num_scalar_prefetch=1, grid=(d // kb,),
            in_specs=[pl.BlockSpec((b, kb), lambda i, m: (0, i)), pl.BlockSpec((kb, cols), lambda i, m: (i, m[0]))],
            out_specs=pl.BlockSpec((b, cols), lambda i, m: (0, 0))),
        out_shape=jax.ShapeDtypeStruct((b, cols), jnp.float32),
        cost_estimate=pl.CostEstimate(flops=2 * b * d * cols, bytes_accessed=2 * d * cols, transcendentals=0),
    )(me[None], cond, w)


def order_kernel(w_ref, hot_ref, o_ref):
    d_local = w_ref.shape[2]
    for c in range(2):
        for h in range(d_local // HEAD):
            at = slice(h * HEAD, (h + 1) * HEAD)
            o_ref[:, c * d_local + h * HEAD:c * d_local + (h + 1) * HEAD] = jnp.dot(
                w_ref[c, :, at], hot_ref[...], preferred_element_type=jnp.float32).astype(o_ref.dtype)
    o_ref[:, 2 * d_local:3 * d_local] = w_ref[2]
    o_ref[:, 3 * d_local:] = jnp.zeros((o_ref.shape[0], o_ref.shape[1] - 3 * d_local), o_ref.dtype)


def order_call(w, hot, rb=512):
    _, d, d_local = w.shape
    cols = -(-3 * d_local // 256) * 256
    return pl.pallas_call(
        order_kernel, grid=(d // rb,),
        in_specs=[pl.BlockSpec((3, rb, d_local), lambda i: (0, i, 0)), pl.BlockSpec((HEAD, HEAD), lambda i: (0, 0))],
        out_specs=pl.BlockSpec((rb, cols), lambda i: (i, 0)),
        out_shape=jax.ShapeDtypeStruct((d, cols), w.dtype),
        cost_estimate=pl.CostEstimate(flops=4 * d * d_local * HEAD, bytes_accessed=12 * d * d_local, transcendentals=0),
    )(w, hot)


def rope_rows(grid_hw, seq_len, sizes):
    tok_idx = jnp.arange(seq_len, dtype=jnp.int32)
    grid_h, grid_w = grid_hw[0], grid_hw[1]
    video = (tok_idx < seq_len - TXT).astype(jnp.int32)
    pos = (tok_idx // (grid_h * grid_w), (tok_idx // grid_w) % grid_h, tok_idx % grid_w)
    lane = jnp.arange(2 * HEAD, dtype=jnp.int32)[None, :]
    hit, start = None, 0
    for p, size in zip(pos, sizes):
        here = lane == (p * video + start)[:, None]
        hit = here if hit is None else hit | here
        start += size
    return hit.astype(jnp.bfloat16)


def rope_table(sizes):
    pair_idx = jnp.arange(HEAD // 2, dtype=jnp.int32)
    axis_sel = (pair_idx >= 8).astype(jnp.int32) + (pair_idx >= 36).astype(jnp.int32)
    within = pair_idx - jnp.where(axis_sel == 0, 0, jnp.where(axis_sel == 1, 8, 36))
    inv_freq = jnp.power(THETA, -2.0 * within.astype(jnp.float32) / jnp.where(axis_sel == 0, 16.0, 56.0))
    row = jnp.arange(2 * HEAD, dtype=jnp.int32)[:, None]
    start, table = 0, jnp.zeros((2 * HEAD, 2 * HEAD), jnp.float32)
    for axis, size in enumerate(sizes):
        angles = (row - start).astype(jnp.float32) * inv_freq
        cos_t, sin_t = jnp.cos(angles), jnp.sin(angles)
        live = (row >= start) & (row < start + size) & (jnp.tile(axis_sel, 4)[None, :] == axis)
        table = jnp.where(live, jnp.concatenate([cos_t, cos_t, -sin_t, sin_t], axis=1), table)
        start += size
    top = table.astype(jnp.bfloat16)
    rest = table - top.astype(jnp.float32)
    mid = rest.astype(jnp.bfloat16)
    low = (rest - mid.astype(jnp.float32)).astype(jnp.bfloat16)
    return jnp.concatenate([top, mid, low], axis=1)


def modulated_norm(tokens, shift, scale):
    tok_f32 = tokens.astype(jnp.float32)
    centered = tok_f32 - jnp.mean(tok_f32, axis=-1, keepdims=True)
    variance = jnp.mean(centered * centered, axis=-1, keepdims=True)
    normed = centered * lax.rsqrt(variance + EPS)
    return (normed * (1.0 + scale) + shift).astype(jnp.bfloat16)


def split_pairs(x):
    s = x.shape
    return jnp.swapaxes(x.reshape(s[:-1] + (s[-1] // HEAD, HEAD // 2, 2)), -1, -2).reshape(s)


def solution(mesh):
    n_tp, n_dp = mesh.shape['tp'], mesh.shape['dp']
    n_x = n_tp // 2
    twin = [(i, i ^ 1) for i in range(n_dp)]
    core = [(i, i ^ 1) for i in range(n_tp)]

    def block_step(tokens, cond_vec, txt_len, grid_hw, w_mod, b_mod, w_qkv, b_qkv, q_gain, k_gain, w_mlp_in, b_mlp_in, w_out_attn, w_out_mlp, b_out):
        batch, rows, d_model = tokens.shape
        seq = rows * n_tp
        d_local = w_qkv.shape[2]
        heads = d_local // HEAD
        width = 128
        n_blk = w_mlp_in.shape[1] // width
        half = n_blk // 2
        side = lax.axis_index('dp') % 2
        me = lax.axis_index('tp')
        cpos, xpos = me % 2, me // 2

        def after(x, *deps):
            return lax.optimization_barrier((x,) + deps)[0]

        def gather(a, tiled=False):
            return lax.all_gather(a, 'tp', axis=0, tiled=tiled)

        def gather_small(a):
            a, step = a[None], 1
            while step < n_tp:
                b = lax.ppermute(a, 'tp', [(i, i ^ step) for i in range(n_tp)])
                a = jnp.where((me // step) % 2 == 0, jnp.concatenate([a, b]), jnp.concatenate([b, a]))
                step *= 2
            return a

        swap = lambda a: lax.ppermute(a, 'tp', core)
        cross = lambda a: lax.ppermute(a, 'dp', twin)
        mine = side * half
        theirs = half - mine
        chunks = ((0, 2), (2, 2), (4, 2))
        pack = lambda first, count, *deps: pack_call(after(first, *deps), count, w_mlp_in, w_out_mlp, width)
        packs = [pack(mine, chunks[0][1])]

        n_mod = w_mod.shape[1] // n_tp
        mod_part = mod_call(after(me, packs[0]), jax.nn.silu(cond_vec).astype(jnp.bfloat16), w_mod, n_mod)
        small = gather_small(jnp.concatenate([mod_part.reshape(-1), b_mlp_in]))
        own_pack = pack(theirs, half, mod_part)[None]
        mate_pack = swap(own_pack)
        for b0, nb in chunks[1:]:
            packs.append(pack(mine + b0, nb, own_pack))
        mod_all = jnp.swapaxes(small[:, :batch * n_mod].reshape(n_tp, batch, n_mod), 0, 1).reshape(batch, -1) + b_mod
        shift, scale, gate = mod_all[:, :d_model], mod_all[:, d_model:2 * d_model], mod_all[:, 2 * d_model:]
        bias = small[:, batch * n_mod:].reshape(n_tp, n_blk, width)
        bias_g = lax.dynamic_slice_in_dim(bias, mine, half, 1)
        bias_n = lax.dynamic_slice_in_dim(bias, theirs, half, 1)
        y_own = [modulated_norm(tokens[s], shift[s], scale[s]) for s in range(batch)]
        y_full = [gather(y_own[s], tiled=True) for s in range(batch)]
        l_pack = [gather(packs[i]) for i in range(len(chunks))]
        w_oa = gather(w_out_attn, tiled=True)

        far_ids = jnp.stack([2 * ((xpos + j) % n_x) + cpos for j in range(1, n_x)])
        near_ids = [2 * ((xpos + j) % n_x) + 1 - cpos for j in range(1, n_x)]
        perm = jnp.arange(HEAD)
        perm = (perm % (HEAD // 2)) * 2 + perm // (HEAD // 2)
        one_hot = (jnp.arange(HEAD)[:, None] == perm[None, :]).astype(jnp.bfloat16)
        w_all = order_call(jnp.swapaxes(w_qkv, 0, 1), one_hot)
        b_all = jnp.concatenate([split_pairs(b_qkv[:2]).reshape(-1), b_qkv[2], jnp.zeros((w_all.shape[1] - 3 * d_local,), jnp.float32)])[None]
        gains = split_pairs(jnp.stack([q_gain, k_gain]))
        sizes = (16, 96, 96)
        table = rope_table(sizes)
        hots = [rope_rows(grid_hw[s], seq, sizes) for s in range(batch)]

        own = (own_pack, lax.dynamic_index_in_dim(bias_n, me, 0))
        mate = (mate_pack, lax.dynamic_index_in_dim(bias_n, me ^ 1, 0))
        left, far, near, qkv, att, spread = {}, {}, {}, {}, {}, {}
        state = {'last': None, 'acc': None, 'out': None}

        def turn(x):
            return x if state['last'] is None else after(x, state['last'])

        def do_send(i):
            b0, nb = chunks[i]
            left[i] = (l_pack[i], bias_g[:, b0:b0 + nb])
            state['last'] = pick_call(far_ids, turn(l_pack[i]))
            far[i] = (cross(state['last']), jnp.stack([bias_n[2 * ((xpos + j) % n_x) + cpos, b0:b0 + nb] for j in range(1, n_x)]))

        def do_relay(i):
            b0, nb = chunks[i]
            near[i] = (swap(turn(far[i][0])), jnp.stack([bias_n[j, b0:b0 + nb] for j in near_ids]))

        def do_qkv(s):
            qkv[s] = qkv_call(turn(y_full[s]), w_all, b_all, gains, hots[s], table, d_local)
            state['last'] = qkv[s][0]

        def do_attend(s):
            q, k, v, stats = qkv[s]
            top = jnp.max(stats, axis=(0, 2))
            bound = jnp.sqrt(top[:heads] * top[heads:2 * heads]) * (SCORE_EXP2 * 1.02) + 1.0
            v_top = top[2 * heads:3 * heads]
            fast = (bound < 100.0) & (v_top * jnp.exp2(bound) < 2.0 ** 110)
            info = jnp.concatenate([(seq - TXT + txt_len[s])[None], fast.astype(jnp.int32)])
            att[s] = attn_call(info, turn(q), k, v)
            state['last'] = att[s]
            spread[s] = lax.all_to_all(att[s].reshape(n_tp, rows, d_local), 'tp', 0, 0, tiled=False)

        def do_mlp(names, proj=(), final=(), ts=tuple(range(batch))):
            stacks, flat = [], []
            for name in names:
                i = int(name[1:] or 0)
                for stack in {'O': (own, mate), 'L': (left.get(i),), 'D': (far.get(i), near.get(i))}[name[0]]:
                    stacks.append(stack)
                    n_shards, _, nb = stack[0].shape[:3]
                    flat += [(len(stacks) - 1, j, b, 2) for j in range(n_shards) for b in range(0, nb, 2)]
            steps = [flat[i:i + 2] for i in range(0, len(flat), 2)]
            y = [y_own[t] for t in ts]
            acc = state['acc'] and [state['acc'][t] for t in ts]
            if acc:
                acc[0] = turn(acc[0])
            elif steps:
                y[0] = turn(y[0])
            tail = (tokens.reshape(batch * rows, d_model), gate, b_out[None], state['out'])
            accs, out = mlp_call(ts, y, acc, stacks, steps, proj=proj, att=[spread[t] for t in proj], w_oa=w_oa, final=final, tail=tail)
            left_over = [t for t in ts if t not in final]
            state['acc'] = {**(state['acc'] or {}), **dict(zip(left_over, accs))}
            if out is not None:
                state['out'] = out
            state['last'] = (accs + [out])[0]

        do_mlp(['O'])
        state['last'] = after(state['last'], w_all, *hots)
        do_send(0)
        do_mlp(['L0'])
        do_qkv(0)
        do_attend(0)
        do_relay(0)
        do_send(1)
        do_mlp(['L1'])
        do_send(2)
        do_mlp(['D0', 'L2'])
        do_relay(1)
        do_qkv(1)
        do_attend(1)
        do_mlp(['D1'])
        do_qkv(2)
        do_relay(2)
        do_attend(2)
        do_mlp(['D2'], proj=(0, 1), final=(0, 1))
        do_mlp([], proj=(2,), final=(2,), ts=(2,))
        return state['out'].reshape(batch, rows, d_model)

    in_specs = (P('dp', 'tp', None), P('dp', None), P('dp'), P('dp', None), P(None, None), P(None), P(None, None, 'tp'), P(None, 'tp'), P(None), P(None), P(None, 'tp'), P('tp'), P('tp', None), P('tp', None), P(None))
    return jax.shard_map(block_step, mesh=mesh, in_specs=in_specs, out_specs=P('dp', 'tp', None), check_vma=False)
```

time: 2600 us -> 1020 us (0.39)
  matrix products: 1090 us -> 0 us
  waiting for transfers between devices: 1030 us -> 155 us
  Pallas kernels: 0 us -> 737 us
  other arithmetic: 303 us -> 51.2 us
  local copies, waits for them, and re-layouts: 150 us -> 11.8 us
    dot_general x21 -> x0, matrix products: 743 us -> none  [the longest x16 288 us: one_block(): jnp.einsum('bhqk,bkhd->bqhd', probs, v_heads, preferred_element_type=jnp....]
    pallas_call x0 -> x22, Pallas kernels: none -> 737 us  [the longest x7 371 us: mlp_call(): pl.pallas_call(functools.partial(mlp_kernel, ts=tuple(ts), steps=steps, n...]
    reduce_scatter x1 -> x0, waiting for transfers between devices: 717 us -> none  [local_step(): own_sum = lax.psum_scatter(part_sum, 'tp', scatter_dimension=1, tiled=True)]
    sub x16 -> x0, matrix products: 350 us -> none  [one_block(): probs = jax.nn.softmax(scores, axis=-1).astype(jnp.bfloat16)]
    all_gather x1 -> x7, waiting for transfers between devices: 309 us -> 89.7 us  [gather(): return lax.all_gather(a, 'tp', axis=0, tiled=tiled)]
    another operation x3 -> x4, other arithmetic: 103 us -> 2.39 us  [the longest x3 1.79 us: do_send(): jnp.stack([bias_n[2 * ((xpos + j) % n_x) + cpos, b0:b0 + nb] for j in ran...]
    mul x2 -> x3, other arithmetic: 71.4 us -> 0.63 us  [rope_rows(): here = lane == (p * video + start)[:, None]]
    another operation x3 -> x8, local copies, waits for them, and re-layouts: 59.8 us -> 0.52 us  [the longest x4 0.41 us: block_step(): gains = split_pairs(jnp.stack([q_gain, k_gain]))]
  transfers between devices with their start and end apart: 2 -> 20, of which waited for: 2 -> 9; matrix products, arithmetic and copies ran while one was open for 1% -> 6% of each run, Pallas kernels for 0% -> 71%
where the time goes in v1:
time: 1020 us; the launch traced here: 1010 us
  Pallas kernels  737 us (72%)
  waiting for transfers between devices  155 us (15%)
  other arithmetic  51.2 us (5%)
  between operations  29.9 us (3%)
  starting transfers between devices  26.5 us (3%)
  local copies, waits for them, and re-layouts  11.8 us (1%)
    pallas_call x7, Pallas kernels, mlp_call(): pl.pallas_call(functools.partial(mlp_kernel, ts=tuple(ts), steps=steps, n...  371 us
    pallas_call x3, Pallas kernels, attn_call(): pl.pallas_call(functools.partial(attn_kernel, sub=sub, bk=bk), grid_spec=...  179 us
    pallas_call x3, Pallas kernels, qkv_call(): pl.pallas_call(functools.partial(qkv_kernel, sub=sub), grid=(steps,), in_...  127 us
    all_gather x7, waiting for transfers between devices, gather(): return lax.all_gather(a, 'tp', axis=0, tiled=tiled)  89.7 us
    all_to_all x3, waiting for transfers between devices, do_attend(): lax.all_to_all(att[s].reshape(n_tp, rows, d_local), 'tp', 0, 0, tiled=False)  35.9 us
    pallas_call x3, Pallas kernels, pick_call(): pl.pallas_call(pick_kernel, grid_spec=pltpu.PrefetchScalarGridSpec(num_sc...  27 us
  transfers between devices with their start and end apart: 20, of which 9 were waited for; matrix products, arithmetic and copies ran while one was open for 6% of the time, Pallas kernels for 71%

profile of v1, /device:TPU:112, one launch (start us, length us, event | category | flops | bytes accessed | tf_op | source)
XLA Modules:
  0.0 1011.5 jit_solution(6366551828697590370)
XLA Ops:
  6.6 3.4 shard_map.145
  10.7 5.0 shard_map.146
  16.6 5.9 convert_reduce_fusion
  22.5 7.1 fusion.17
  29.7 2.4 collective-permute-start.1
  32.0 3.2 collective-permute-done.1
  35.3 3.6 collective-permute-start.2
  38.9 4.7 collective-permute-done.2
  44.5 9.2 fusion.20
  53.9 9.2 shard_map.147
  63.1 3.5 shard_map.151
  66.8 3.4 shard_map.157
  81.6 8.4 shard_map.152.w_ref
  92.0 1.4 multiply_cosine_fusion.2
  94.8 4.6 fusion.23.hot_ref
  101.8 42.3 %shard_map.148 = (f32[512,3072]{1,0:T(8,128)}, f32[512,3072]{1,0:T(8,128)}, f32[512,3072]{1,0:T(8,128)}) custom-call(bf16[512,3072]{1,0:T(8,128)(2,1)} %get-tuple-element.109.refs_0_, bf16[512,3072]{1,0:T(8,128)(2,1)} %get-tuple-element.108.refs_1_, bf16[512,3072]{1,0:T(8,128)(2,1)} %get-tuple-element.107.refs_2_, bf16[1,2,6,128,3072]{4,3,2,1,0:T(8,128)(2,1)} %bitcast.119, ...), custom_call_target="tpu_custom_call" | custom-call | flops 28991029248 | bytes 66060288 | tf_op jit(solution)/shard_map/pallas_call | solution.py:402
  144.2 9.3 shard_map.149
  153.5 2.0 collective-permute-start.4
  155.6 54.9 %shard_map.150 = (f32[512,3072]{1,0:T(8,128)}, f32[512,3072]{1,0:T(8,128)}, f32[512,3072]{1,0:T(8,128)}) custom-call(bf16[512,3072]{1,0:T(8,128)(2,1)} %get-tuple-element.109.refs_0_, bf16[512,3072]{1,0:T(8,128)(2,1)} %get-tuple-element.108.refs_1_, bf16[512,3072]{1,0:T(8,128)(2,1)} %get-tuple-element.107.refs_2_, f32[512,3072]{1,0:T(8,128)} %get-tuple-element.55.refs_3_, ...), custom_call_target="tpu_custom_call" | custom-call | flops 38654705664 | bytes 72351744 | tf_op jit(solution)/shard_map/pallas_call | solution.py:402
  210.5 39.9 %all-gather.11.cloned.1.call-done.y_ref = bf16[4096,3072]{1,0:T(8,128)(2,1)} async-done(((bf16[512,3072]{1,0:T(8,128)(2,1)}), bf16[4096,3072]{1,0:T(8,128)(2,1)}) %all-gather.11.cloned.1.call-update) | async-done | bytes 25165840 | tf_op jit(solution)/shard_map/all_gather | solution.py:570
  250.4 42.2 %shard_map.153 = (bf16[4096,384]{1,0:T(8,128)(2,1)}, bf16[4096,384]{1,0:T(8,128)(2,1)}, bf16[4096,384]{1,0:T(8,128)(2,1)}, f32[8,16,128]{2,1,0:T(8,128)}) custom-call(bf16[4096,3072]{1,0:T(8,128)(2,1)} %all-gather.11.cloned.1.call-done.y_ref, bf16[3072,1280]{1,0:T(8,128)(2,1)} %shard_map.152.w_ref, f32[1,1280]{1,0:T(1,128)} %broadcast_in_dim.43.b_ref, ...), custom_call_target="tpu_custom_call" | custom-call | flops 32212254720 | bytes 35651584 | tf_op jit(solution)/shard_map/pallas_call | solution.py:63
  294.3 59.9 %shard_map.154 = bf16[4096,384]{1,0:T(8,128)(2,1)} custom-call(s32[4]{0:T(128)} %pad_add_fusion.1.info_ref, bf16[4096,384]{1,0:T(8,128)(2,1)} %get-tuple-element.62.q_ref, bf16[4096,384]{1,0:T(8,128)(2,1)} %get-tuple-element.63.k_ref, bf16[4096,384]{1,0:T(8,128)(2,1)} %get-tuple-element.64.v_ref), custom_call_target="tpu_custom_call" | custom-call | flops 51539607552 | bytes 12582912 | tf_op jit(solution)/shard_map/pallas_call | solution.py:152
  354.2 5.1 collective-permute-done.4.refs_6_
  369.9 4.7 fusion.26.hot_ref
  375.8 1.7 constant_dynamic-slice_fusion.4
  378.1 9.7 shard_map.155
  387.7 1.5 collective-permute-start.6
  389.2 55.3 %shard_map.156 = (f32[512,3072]{1,0:T(8,128)}, f32[512,3072]{1,0:T(8,128)}, f32[512,3072]{1,0:T(8,128)}) custom-call(bf16[512,3072]{1,0:T(8,128)(2,1)} %get-tuple-element.109.refs_0_, bf16[512,3072]{1,0:T(8,128)(2,1)} %get-tuple-element.108.refs_1_, bf16[512,3072]{1,0:T(8,128)(2,1)} %get-tuple-element.107.refs_2_, f32[512,3072]{1,0:T(8,128)} %get-tuple-element.66.refs_3_, ...), custom_call_target="tpu_custom_call" | custom-call | flops 38654705664 | bytes 72351744 | tf_op jit(solution)/shard_map/pallas_call | solution.py:402
  444.6 43.6 %all-gather.23.cloned.1.call-done = bf16[16,2,128,3072]{3,2,1,0:T(8,128)(2,1)} async-done(((bf16[2,2,128,3072]{3,2,1,0:T(8,128)(2,1)}), bf16[16,2,128,3072]{3,2,1,0:T(8,128)(2,1)}) %all-gather.23.cloned.1.call-update) | async-done | bytes 25165840 | tf_op jit(solution)/shard_map/all_gather | solution.py:570
  488.2 8.0 shard_map.158
  496.2 90.1 %shard_map.159 = (f32[512,3072]{1,0:T(8,128)}, f32[512,3072]{1,0:T(8,128)}, f32[512,3072]{1,0:T(8,128)}) custom-call(bf16[512,3072]{1,0:T(8,128)(2,1)} %get-tuple-element.109.refs_0_, bf16[512,3072]{1,0:T(8,128)(2,1)} %get-tuple-element.108.refs_1_, bf16[512,3072]{1,0:T(8,128)(2,1)} %get-tuple-element.107.refs_2_, f32[512,3072]{1,0:T(8,128)} %get-tuple-element.72.refs_3_, ...), custom_call_target="tpu_custom_call" | custom-call | flops 67645734912 | bytes 91226112 | tf_op jit(solution)/shard_map/pallas_call | solution.py:402
  586.3 7.0 collective-permute-done.6.refs_6_
  594.8 4.6 fusion.29.hot_ref
  600.0 1.6 collective-permute-start.8
  601.6 6.1 all-gather.13.cloned.1.call-done.y_ref
  607.8 42.6 %shard_map.160 = (bf16[4096,384]{1,0:T(8,128)(2,1)}, bf16[4096,384]{1,0:T(8,128)(2,1)}, bf16[4096,384]{1,0:T(8,128)(2,1)}, f32[8,16,128]{2,1,0:T(8,128)}) custom-call(bf16[4096,3072]{1,0:T(8,128)(2,1)} %all-gather.13.cloned.1.call-done.y_ref, bf16[3072,1280]{1,0:T(8,128)(2,1)} %shard_map.152.w_ref, f32[1,1280]{1,0:T(1,128)} %broadcast_in_dim.43.b_ref, ...), custom_call_target="tpu_custom_call" | custom-call | flops 32212254720 | bytes 35651584 | tf_op jit(solution)/shard_map/pallas_call | solution.py:63
  652.0 59.6 %shard_map.161 = bf16[4096,384]{1,0:T(8,128)(2,1)} custom-call(s32[4]{0:T(128)} %pad_add_fusion.2.info_ref, bf16[4096,384]{1,0:T(8,128)(2,1)} %get-tuple-element.79.q_ref, bf16[4096,384]{1,0:T(8,128)(2,1)} %get-tuple-element.80.k_ref, bf16[4096,384]{1,0:T(8,128)(2,1)} %get-tuple-element.81.v_ref), custom_call_target="tpu_custom_call" | custom-call | flops 51539607552 | bytes 12582912 | tf_op jit(solution)/shard_map/pallas_call | solution.py:152
  711.6 43.8 %shard_map.162 = (f32[512,3072]{1,0:T(8,128)}, f32[512,3072]{1,0:T(8,128)}, f32[512,3072]{1,0:T(8,128)}) custom-call(bf16[512,3072]{1,0:T(8,128)(2,1)} %get-tuple-element.109.refs_0_, bf16[512,3072]{1,0:T(8,128)(2,1)} %get-tuple-element.108.refs_1_, bf16[512,3072]{1,0:T(8,128)(2,1)} %get-tuple-element.107.refs_2_, f32[512,3072]{1,0:T(8,128)} %get-tuple-element.82.refs_3_, ...), custom_call_target="tpu_custom_call" | custom-call | flops 28991029248 | bytes 66060288 | tf_op jit(solution)/shard_map/pallas_call | solution.py:402
  755.4 42.3 %shard_map.163 = (bf16[4096,384]{1,0:T(8,128)(2,1)}, bf16[4096,384]{1,0:T(8,128)(2,1)}, bf16[4096,384]{1,0:T(8,128)(2,1)}, f32[8,16,128]{2,1,0:T(8,128)}) custom-call(bf16[4096,3072]{1,0:T(8,128)(2,1)} %all-gather.15.cloned.1.call-done.y_ref, bf16[3072,1280]{1,0:T(8,128)(2,1)} %shard_map.152.w_ref, f32[1,1280]{1,0:T(1,128)} %broadcast_in_dim.43.b_ref, ...), custom_call_target="tpu_custom_call" | custom-call | flops 32212254720 | bytes 35651584 | tf_op jit(solution)/shard_map/pallas_call | solution.py:63
  797.7 7.9 collective-permute-done.8.refs_6_
  805.7 4.6 all-to-all-start
  810.9 1.4 slice.171.refs_14_.refs_4_
  813.9 35.9 %all-to-all-done.refs_10_ = bf16[8,512,384]{2,1,0:T(8,128)(2,1)} async-done(((bf16[8,512,384]{2,1,0:T(8,128)(2,1)}), bf16[8,512,384]{2,1,0:T(8,128)(2,1)}, u32[]{:S(2)}, u32[]{:S(2)}) %all-to-all-start) | async-done | bytes 3145760 | tf_op jit(solution)/shard_map/all_to_all | solution.py:648
  849.8 4.9 all-to-all-start.1
  854.7 59.6 %shard_map.164 = bf16[4096,384]{1,0:T(8,128)(2,1)} custom-call(s32[4]{0:T(128)} %pad_add_fusion.3.info_ref, bf16[4096,384]{1,0:T(8,128)(2,1)} %get-tuple-element.90.q_ref, bf16[4096,384]{1,0:T(8,128)(2,1)} %get-tuple-element.91.k_ref, bf16[4096,384]{1,0:T(8,128)(2,1)} %get-tuple-element.92.v_ref), custom_call_target="tpu_custom_call" | custom-call | flops 51539607552 | bytes 12582912 | tf_op jit(solution)/shard_map/pallas_call | solution.py:152
  914.2 5.1 all-to-all-start.2
  919.4 66.0 %shard_map.165 = (f32[512,3072]{1,0:T(8,128)}, bf16[1536,3072]{1,0:T(8,128)(2,1)}) custom-call(bf16[512,3072]{1,0:T(8,128)(2,1)} %get-tuple-element.109.refs_0_, bf16[512,3072]{1,0:T(8,128)(2,1)} %get-tuple-element.108.refs_1_, bf16[512,3072]{1,0:T(8,128)(2,1)} %get-tuple-element.107.refs_2_, f32[512,3072]{1,0:T(8,128)} %get-tuple-element.93.refs_3_, ...), custom_call_target="tpu_custom_call" | custom-call | flops 48318382080 | bytes 66060288 | tf_op jit(solution)/shard_map/pallas_call | solution.py:402
  985.4 18.7 %shard_map.166 = bf16[1536,3072]{1,0:T(8,128)(2,1)} custom-call(f32[512,3072]{1,0:T(8,128)} %get-tuple-element.97.refs_0_, bf16[8,512,384]{2,1,0:T(8,128)(2,1)} %all-to-all-done.2.refs_1_, bf16[3,2,4,128,3072]{4,3,2,1,0:T(8,128)(2,1)} %bitcast.117, bf16[1536,3072]{1,0:T(8,128)(2,1)} %bitcast.109, ...), custom_call_target="tpu_custom_call", output_to_operand_aliasing={{}: (6, {})} | custom-call | flops 9663676416 | bytes 15728640 | tf_op jit(solution)/shard_map/pallas_call | solution.py:402
  (147 shorter events, 24.6 us)
Async XLA Ops:
  6.5 137.6 %all-gather.19.cloned.1.call-start = ((), (), s32[]{:S(2)}) async-start(), calls=%async_computation.7 | async-start | bytes 28311552 | tf_op jit(solution)/shard_map/all_gather | solution.py:570
  6.6 3.5 copy-start.3
  10.0 240.4 %all-gather.11.cloned.1.call-start = ((), (), s32[]{:S(2)}) async-start(), calls=%async_computation.3 | async-start | bytes 28311552 | tf_op jit(solution)/shard_map/all_gather | solution.py:570
  10.7 5.7 copy-start.9
  16.5 13.1 %collective-permute-start = (f32[1,4992]{1,0:T(1,128)S(1)}, f32[1,4992]{1,0:T(1,128)S(1)}, u32[]{:S(2)}, u32[]{:S(2)}) collective-permute-start(f32[1,4992]{1,0:T(1,128)S(1)} %broadcast_in_dim.38), channel_id=1, source_target_pairs={{0,1},{1,0},{2,3},{3,2},{4,5},{5,4},{6,7},{7,6},{8,9},{9,8},{10,11... | collective-permute-start | bytes 59912 | tf_op jit(solution)/shard_map/ppermute | solution.py:575
  22.5 21.3 %copy-start.4 = (f32[9216]{0:T(1024)S(1)}, f32[9216]{0:T(1024)}, u32[]{:S(2)}) copy-start(f32[9216]{0:T(1024)} %param.20) | copy-start | bytes 110596
  29.7 5.6 collective-permute-start.1
  35.3 8.3 collective-permute-start.2
  43.8 0.7 copy-start
  53.8 324.3 %all-gather.21.cloned.1.call-start = ((), (), s32[]{:S(2)}) async-start(), calls=%async_computation.8 | async-start | bytes 28311552 | tf_op jit(solution)/shard_map/all_gather | solution.py:570
  66.7 421.5 %all-gather.23.cloned.1.call-start = ((), (), s32[]{:S(2)}) async-start(), calls=%async_computation.9 | async-start | bytes 28311552 | tf_op jit(solution)/shard_map/all_gather | solution.py:570
  70.2 1.8 copy-start.8
  70.2 7.5 slice-start
  70.2 7.9 copy-start.7
  70.2 8.5 copy-start.17
  70.2 8.7 copy-start.18
  70.2 9.6 copy-start.10
  70.3 537.5 %all-gather.13.cloned.1.call-start = ((), (), s32[]{:S(2)}) async-start(), calls=%async_computation.4 | async-start | bytes 28311552 | tf_op jit(solution)/shard_map/all_gather | solution.py:570
  70.9 684.5 %all-gather.15.cloned.1.call-start = ((), (), s32[]{:S(2)}) async-start(), calls=%async_computation.5 | async-start | bytes 28311552 | tf_op jit(solution)/shard_map/all_gather | solution.py:570
  71.6 847.8 %all-gather.17.cloned.1.call-start = ((), (), s32[]{:S(2)}) async-start(), calls=%async_computation.6 | async-start | bytes 21233664 | tf_op jit(solution)/shard_map/all_gather | solution.py:570
  71.8 30.0 %collective-permute-start.3 = (bf16[1,2,6,128,3072]{4,3,2,1,0:T(8,128)(2,1)}, bf16[1,2,6,128,3072]{4,3,2,1,0:T(8,128)(2,1)}, u32[]{:S(2)}, u32[]{:S(2)}) collective-permute-start(bf16[1,2,6,128,3072]{4,3,2,1,0:T(8,128)(2,1)} %bitcast.118), channel_id=1, source_target_pairs={{0,1},{1,0},{2,3},{3,2},{4,5},{5,4},{6,7},{7,6},{8,9},{9,8},{10,11... | collective-permute-start | bytes 28311560 | tf_op jit(solution)/shard_map/ppermute | solution.py:580
  99.4 1.2 copy-start.1
  153.5 205.7 %collective-permute-start.4 = (bf16[3,2,2,128,3072]{4,3,2,1,0:T(8,128)(2,1)}, bf16[3,2,2,128,3072]{4,3,2,1,0:T(8,128)(2,1)}, u32[]{:S(2)}, u32[]{:S(2)}) collective-permute-start(bf16[3,2,2,128,3072]{4,3,2,1,0:T(8,128)(2,1)} %shard_map.149), channel_id=1, source_target_pairs={{0,8},{8,0},{1,9},{9,1},{2,10},{10,2},{3,11},{11,3},{4,12},{12,4},... | collective-permute-start | bytes 28311560 | tf_op jit(solution)/shard_map/ppermute | solution.py:581
  294.3 80.3 %copy-start.6 = (f32[8,2,128]{2,0,1:T(8,128)S(1)}, f32[8,2,128]{2,0,1:T(8,128)}, u32[]{:S(2)}) copy-start(f32[8,2,128]{2,0,1:T(8,128)} %get-tuple-element.137) | copy-start | bytes 24580
  294.3 80.9 %copy-start.5 = (f32[8,2,128]{2,0,1:T(8,128)S(1)}, f32[8,2,128]{2,0,1:T(8,128)}, u32[]{:S(2)}) copy-start(f32[8,2,128]{2,0,1:T(8,128)} %get-tuple-element.136) | copy-start | bytes 24580
  359.3 136.9 %collective-permute-start.5 = (bf16[3,2,2,128,3072]{4,3,2,1,0:T(8,128)(2,1)}, bf16[3,2,2,128,3072]{4,3,2,1,0:T(8,128)(2,1)}, u32[]{:S(2)}, u32[]{:S(2)}) collective-permute-start(bf16[3,2,2,128,3072]{4,3,2,1,0:T(8,128)(2,1)} %collective-permute-done.4.refs_6_), channel_id=1, source_target_pairs={{0,1},{1,0},{2,3},{3,2},{4,5},{5,4},{6,7},{7,6},{8,9},{9,8},{10,11... | collective-permute-start | bytes 28311560 | tf_op jit(solution)/shard_map/ppermute | solution.py:580
  387.7 205.6 %collective-permute-start.6 = (bf16[3,2,2,128,3072]{4,3,2,1,0:T(8,128)(2,1)}, bf16[3,2,2,128,3072]{4,3,2,1,0:T(8,128)(2,1)}, u32[]{:S(2)}, u32[]{:S(2)}) collective-permute-start(bf16[3,2,2,128,3072]{4,3,2,1,0:T(8,128)(2,1)} %shard_map.155), channel_id=1, source_target_pairs={{0,8},{8,0},{1,9},{9,1},{2,10},{10,2},{3,11},{11,3},{4,12},{12,4},... | collective-permute-start | bytes 28311560 | tf_op jit(solution)/shard_map/ppermute | solution.py:581
  593.4 118.2 %collective-permute-start.7 = (bf16[3,2,2,128,3072]{4,3,2,1,0:T(8,128)(2,1)}, bf16[3,2,2,128,3072]{4,3,2,1,0:T(8,128)(2,1)}, u32[]{:S(2)}, u32[]{:S(2)}) collective-permute-start(bf16[3,2,2,128,3072]{4,3,2,1,0:T(8,128)(2,1)} %collective-permute-done.6.refs_6_), channel_id=1, source_target_pairs={{0,1},{1,0},{2,3},{3,2},{4,5},{5,4},{6,7},{7,6},{8,9},{9,8},{10,11... | collective-permute-start | bytes 28311560 | tf_op jit(solution)/shard_map/ppermute | solution.py:580
  600.0 205.7 %collective-permute-start.8 = (bf16[3,2,2,128,3072]{4,3,2,1,0:T(8,128)(2,1)}, bf16[3,2,2,128,3072]{4,3,2,1,0:T(8,128)(2,1)}, u32[]{:S(2)}, u32[]{:S(2)}) collective-permute-start(bf16[3,2,2,128,3072]{4,3,2,1,0:T(8,128)(2,1)} %shard_map.158), channel_id=1, source_target_pairs={{0,8},{8,0},{1,9},{9,1},{2,10},{10,2},{3,11},{11,3},{4,12},{12,4},... | collective-permute-start | bytes 28311560 | tf_op jit(solution)/shard_map/ppermute | solution.py:581
  797.7 14.7 %copy-start.11 = (f32[1,2,128]{2,0,1:T(1,128)S(1)}, f32[1,2,128]{2,0,1:T(1,128)}, u32[]{:S(2)}) copy-start(f32[1,2,128]{2,0,1:T(1,128)} %get-tuple-element.118) | copy-start | bytes 3076
  797.7 14.7 %copy-start.12 = (f32[1,2,128]{2,0,1:T(1,128)S(1)}, f32[1,2,128]{2,0,1:T(1,128)}, u32[]{:S(2)}) copy-start(f32[1,2,128]{2,0,1:T(1,128)} %get-tuple-element.119) | copy-start | bytes 3076
  797.7 14.7 %copy-start.13 = (f32[1,2,128]{2,0,1:T(1,128)S(1)}, f32[1,2,128]{2,0,1:T(1,128)}, u32[]{:S(2)}) copy-start(f32[1,2,128]{2,0,1:T(1,128)} %get-tuple-element.120) | copy-start | bytes 3076
  797.7 14.7 %copy-start.14 = (f32[1,2,128]{2,0,1:T(1,128)S(1)}, f32[1,2,128]{2,0,1:T(1,128)}, u32[]{:S(2)}) copy-start(f32[1,2,128]{2,0,1:T(1,128)} %get-tuple-element.121) | copy-start | bytes 3076
  797.7 14.7 %copy-start.15 = (f32[1,2,128]{2,0,1:T(1,128)S(1)}, f32[1,2,128]{2,0,1:T(1,128)}, u32[]{:S(2)}) copy-start(f32[1,2,128]{2,0,1:T(1,128)} %get-tuple-element.122) | copy-start | bytes 3076
  797.7 14.7 %copy-start.16 = (f32[1,2,128]{2,0,1:T(1,128)S(1)}, f32[1,2,128]{2,0,1:T(1,128)}, u32[]{:S(2)}) copy-start(f32[1,2,128]{2,0,1:T(1,128)} %get-tuple-element.135) | copy-start | bytes 3076
  797.7 15.3 %copy-start.2 = (f32[8,16,128]{2,1,0:T(8,128)S(1)}, f32[8,16,128]{2,1,0:T(8,128)}, u32[]{:S(2)}) copy-start(f32[8,16,128]{2,1,0:T(8,128)} %get-tuple-element.88) | copy-start | bytes 196612
  805.6 113.8 %collective-permute-start.9 = (bf16[3,2,2,128,3072]{4,3,2,1,0:T(8,128)(2,1)}, bf16[3,2,2,128,3072]{4,3,2,1,0:T(8,128)(2,1)}, u32[]{:S(2)}, u32[]{:S(2)}) collective-permute-start(bf16[3,2,2,128,3072]{4,3,2,1,0:T(8,128)(2,1)} %collective-permute-done.8.refs_6_), channel_id=1, source_target_pairs={{0,1},{1,0},{2,3},{3,2},{4,5},{5,4},{6,7},{7,6},{8,9},{9,8},{10,11... | collective-permute-start | bytes 28311560 | tf_op jit(solution)/shard_map/ppermute | solution.py:580
  805.7 44.1 %all-to-all-start = ((bf16[8,512,384]{2,1,0:T(8,128)(2,1)}), bf16[8,512,384]{2,1,0:T(8,128)(2,1)}, u32[]{:S(2)}, u32[]{:S(2)}) async-start(bf16[8,512,384]{2,1,0:T(8,128)(2,1)} %bitcast.121), calls=%async_computation | async-start | bytes 6291456 | tf_op jit(solution)/shard_map/all_to_all | solution.py:648
  849.8 64.5 %all-to-all-start.1 = ((bf16[8,512,384]{2,1,0:T(8,128)(2,1)}), bf16[8,512,384]{2,1,0:T(8,128)(2,1)}, u32[]{:S(2)}, u32[]{:S(2)}) async-start(bf16[8,512,384]{2,1,0:T(8,128)(2,1)} %bitcast.34), calls=%async_computation.1 | async-start | bytes 6291456 | tf_op jit(solution)/shard_map/all_to_all | solution.py:648
  914.2 71.1 %all-to-all-start.2 = ((bf16[8,512,384]{2,1,0:T(8,128)(2,1)}), bf16[8,512,384]{2,1,0:T(8,128)(2,1)}, u32[]{:S(2)}, u32[]{:S(2)}) async-start(bf16[8,512,384]{2,1,0:T(8,128)(2,1)} %bitcast.122), calls=%async_computation.2 | async-start | bytes 6291456 | tf_op jit(solution)/shard_map/all_to_all | solution.py:648
Sparse Core Ops, SparseCore 0:
  10.1 121.5 all-gather.18
  133.3 117.0 all-gather.10
  252.0 118.1 all-gather.20
  371.6 116.5 all-gather.22
  489.6 118.0 all-gather.12
  609.2 116.5 all-gather.14
  727.4 93.4 all-gather.16

commit v2 on v1

--- a/solution.py
+++ b/solution.py
@@ -15,6 +15,8 @@
 THETA = 256.0
 NT = (((1,), (1,)), ((), ()))
 LOG2E = math.log2(math.e)
+GELU_0 = math.sqrt(2.0 / math.pi)
+GELU_1 = 0.044715 * GELU_0
 SCORE_EXP2 = HEAD ** -0.5 * LOG2E
 VMEM = 64 * 1024 * 1024 - 128 * 1024
 
@@ -70,7 +72,9 @@
     )(y, w, b, gains, hot, table)
 
 
-def attn_kernel(info_ref, q_ref, k_ref, v_ref, o_ref, p_ref, vx_ref, *, sub, bk):
+def attn_kernel(info_ref, q_ref, k_ref, v_ref, *refs, sub, bk):
+    o_all, p_ref, vx_ref = refs[-3:]
+    per = o_all.shape[2]
     h = pl.program_id(0)
     i = pl.program_id(1)
     n = k_ref.shape[0]
@@ -94,7 +98,7 @@
     def _():
         def weighted(t):
             acc = jnp.dot(p_ref[t % 2], vx_ref[...], preferred_element_type=jnp.float32)
-            o_ref[t * sub:(t + 1) * sub, :] = (acc[:, :HEAD] / acc[:, HEAD:]).astype(jnp.bfloat16)
+            o_all[t * sub // per, 0, t * sub % per:t * sub % per + sub, :] = (acc[:, :HEAD] / acc[:, HEAD:]).astype(jnp.bfloat16)
 
         for t in range(bq // sub):
             q = q_ref[t * sub:(t + 1) * sub, :]
@@ -113,8 +117,8 @@
             vp = jnp.where(pad, v_ref[vid:, :].astype(jnp.float32), 0.0).astype(jnp.bfloat16)
             on = jnp.where(pad, 1.0, 0.0).astype(jnp.bfloat16)
             acc = jnp.dot(p, jnp.concatenate([vp, on], axis=1), preferred_element_type=jnp.float32)
-            old = o_ref[bq - TXT:, :].astype(jnp.float32)
-            o_ref[bq - TXT:, :] = jnp.where(pad, acc[:, :HEAD] / acc[:, HEAD:], old).astype(jnp.bfloat16)
+            old = o_all[bq // per - 1, 0, per - TXT:, :].astype(jnp.float32)
+            o_all[bq // per - 1, 0, per - TXT:, :] = jnp.where(pad, acc[:, :HEAD] / acc[:, HEAD:], old).astype(jnp.bfloat16)
 
     @pl.when(jnp.logical_not(fast))
     def _():
@@ -138,29 +142,32 @@
 
             m0 = jnp.full((bs, 1), -3e38, jnp.float32)
             _, acc = lax.fori_loop(0, n // bs, keys, (m0, jnp.zeros((bs, 2 * HEAD), jnp.float32)))
-            o_ref[pl.ds(r0, bs), :] = (acc[:, :HEAD] / acc[:, HEAD:]).astype(jnp.bfloat16)
+            o_all[lax.div(r0, per), 0, pl.ds(pl.multiple_of(lax.rem(r0, per), bs), bs), :] = (acc[:, :HEAD] / acc[:, HEAD:]).astype(jnp.bfloat16)
             return 0
 
         lax.fori_loop(0, bq // bs, rows, 0)
 
 
-def attn_call(info, q, k, v, bq=1024, sub=512, bk=1024):
+def attn_call(info, q, k, v, rows, slot, slots, out=None, bq=1024, sub=512, bk=1024):
     n, dl = q.shape
     heads = dl // HEAD
     kv = pl.BlockSpec((n, HEAD), lambda h, i, _: (0, h))
-    qo = pl.BlockSpec((bq, HEAD), lambda h, i, _: (i, h))
+    args = [info, q, k, v] + ([] if out is None else [out])
     return pl.pallas_call(
         functools.partial(attn_kernel, sub=sub, bk=bk),
         grid_spec=pltpu.PrefetchScalarGridSpec(
-            num_scalar_prefetch=1, grid=(heads, n // bq), in_specs=[qo, kv, kv], out_specs=qo,
+            num_scalar_prefetch=1, grid=(heads, n // bq),
+            in_specs=[pl.BlockSpec((bq, HEAD), lambda h, i, _: (i, h)), kv, kv] + [pl.BlockSpec(memory_space=pl.ANY)] * (len(args) - 4),
+            out_specs=pl.BlockSpec((bq // rows, 1, rows, HEAD), lambda h, i, _: (i, slot, 0, h)),
             scratch_shapes=[pltpu.VMEM((2, sub, n), jnp.bfloat16), pltpu.VMEM((n, 2 * HEAD), jnp.bfloat16)]),
-        out_shape=jax.ShapeDtypeStruct((n, dl), jnp.bfloat16),
+        out_shape=jax.ShapeDtypeStruct((n // rows, slots, rows, dl), jnp.bfloat16),
+        input_output_aliases={} if out is None else {4: 0},
         compiler_params=pltpu.CompilerParams(vmem_limit_bytes=VMEM),
         cost_estimate=pl.CostEstimate(flops=8 * n * n * dl, bytes_accessed=8 * n * dl, transcendentals=n * n * heads),
-    )(info, q, k, v)
-
-
-def mlp_kernel(*refs, ts, steps, n_stacks, first, proj, final, aliased, nw):
+    )(*args)
+
+
+def mlp_kernel(*refs, ts, steps, n_stacks, first, proj, slots, final, aliased, nw):
     refs = list(refs)
     take = lambda k: [refs.pop(0) for _ in range(k)]
     n = len(ts)
@@ -174,7 +181,7 @@
     accs_out = [t for t in ts if t not in final]
     out_acc = dict(zip(accs_out, take(len(accs_out))))
     out_hbm, = take(1) if final else (None,)
-    y_v, acc_v, w_v, u_v, h_v, bias_v, att_v, tok_v, y_sem, acc_sem, w_sem, out_sem, att_sem, tok_sem = refs
+    y_v, acc_v, w_v, u_v, h_v, bias_v, att_v, tok_v, y_sem, acc_sem, w_sem, out_sem, att_sem, tok_sem, tail_sem = refs
     tb, d_model = acc_v.shape[1:]
     _, _, group, width, _ = w_v.shape
     kdim = group * width
@@ -191,8 +198,8 @@
 
     def att_copies(j):
         att = att_hbm[proj[j]]
-        w = att.shape[2]
-        return [pltpu.make_async_copy(att.at[k], att_v.at[j, :, pl.ds(k * w, w)], att_sem.at[j, k]) for k in range(att.shape[0])]
+        w = att.shape[3]
+        return [pltpu.make_async_copy(att.at[k, slots[j]], att_v.at[j, :, pl.ds(k * w, w)], att_sem.at[j, k]) for k in range(att.shape[0])]
 
     def weight_copies(s, slot, kind):
         if s >= n_steps:
@@ -227,21 +234,34 @@
             u_v[:, at] = lax.dot_general(y_v[t], w, NT, preferred_element_type=jnp.float32) + bias_v[s, :, at]
 
     def act():
-        h_v[...] = jax.nn.gelu(u_v[...], approximate=True).astype(jnp.bfloat16)
-
-    def down(k, slot):
-        t = lax.rem(k, n)
+        u = u_v[...]
+        half = 0.5 * u
+        h_v[...] = (half * jnp.tanh(u * (GELU_1 * (u * u) + GELU_0)) + half).astype(jnp.bfloat16)
+
+    def down(k, slot, store=False):
+        t = n - 1 if store else lax.rem(k, n)
         for c in range(0, d_model, nw):
             w2 = w_v[slot, 1, :, :, c:c + nw].reshape(kdim, nw)
             old = acc_v[t, :, c:c + nw]
             if first:
                 old = jnp.where(k < n, 0.0, old)
             acc_v[t, :, c:c + nw] = old + jnp.dot(h_v[...], w2, preferred_element_type=jnp.float32)
+            if store:
+                tail_store(c).start()
+
+    def tail_store(c):
+        at = pl.ds(c, nw)
+        return pltpu.make_async_copy(acc_v.at[n - 1, :, at], out_acc[ts[n - 1]].at[:, at], tail_sem.at[c // nw])
 
     total = n_steps + n_proj
     if n_steps:
+        for c in weight_copies(0, 0, 0):
+            c.start()
         y_copy(0).start()
-    start_weights(0)
+        for c in weight_copies(0, 0, 1):
+            c.start()
+    else:
+        start_weights(0)
     for s, parts in enumerate(steps):
         at = 0
         for i, shard, b0, nb in parts:
@@ -249,20 +269,25 @@
                 bias_v[s, :, at * width:(at + 1) * width] = bias[i][shard, b:b + 1, :]
                 at += 1
     if n_steps:
+        for c in weight_copies(0, 0, 0):
+            c.wait()
         y_copy(0).wait()
-        arrive(0, 0)
         for i in range(1, n):
             y_copy(i).start()
-    if not first:
-        for i in range(n):
-            acc_copy(i).start()
+        if not first:
+            acc_copy(0).start()
     for j in range(len(proj)):
         for c in att_copies(j):
             c.start()
+    if not first:
+        for i in range(int(bool(n_steps)), n):
+            acc_copy(i).start()
     for t in final:
         tok_copy(ts.index(t)).start()
     if n_steps:
         up(0, 0, 0)
+        for c in weight_copies(0, 0, 1):
+            c.wait()
         last = n * n_steps - 1
 
         def trip(k, _):
@@ -301,9 +326,7 @@
         act()
         if not first and n_steps == 1:
             acc_copy(n - 1).wait()
-        down(last, (n_steps - 1) % 2)
-        if not proj:
-            acc_store(n - 1).start()
+        down(last, (n_steps - 1) % 2, store=not proj)
     elif not first:
         for i in range(n):
             acc_copy(i).wait()
@@ -350,7 +373,11 @@
         for j in range(len(proj)):
             turn(j, 0, closing=True)
     for i, t in enumerate(ts):
-        (out_store if t in final else acc_store)(i).wait()
+        if i == n - 1 and not proj:
+            for c in range(0, d_model, nw):
+                tail_store(c).wait()
+        else:
+            (out_store if t in final else acc_store)(i).wait()
 
 
 def mlp_call(ts, y, acc, stacks, steps, proj=(), att=(), w_oa=None, final=(), tail=None, group=4, nw=512):
@@ -372,7 +399,7 @@
         add(hbm, *acc)
     add(hbm, *[s[0] for s in stacks])
     add(vm, *[s[1] for s in stacks])
-    add(hbm, *att)
+    add(hbm, *[a for a, _ in att])
     if proj:
         add(hbm, w_oa.reshape(d // (2 * group * width), 2, group, width, d))
     alias = {}
@@ -395,12 +422,12 @@
         pltpu.VMEM(has(n_steps, tb, group * width), jnp.float32), pltpu.VMEM(has(n_steps, tb, group * width), jnp.bfloat16),
         pltpu.VMEM((max(1, n_steps), 1, group * width), jnp.float32),
         pltpu.VMEM(has(proj, n_par, tb, d), jnp.bfloat16), pltpu.VMEM(has(final, max(1, len(final)), tb, d), jnp.bfloat16),
-        pltpu.SemaphoreType.DMA((n,)), pltpu.SemaphoreType.DMA((n,)), pltpu.SemaphoreType.DMA((2, 2, 2)), pltpu.SemaphoreType.DMA((n,)),
-        pltpu.SemaphoreType.DMA((n_par, 8)), pltpu.SemaphoreType.DMA((max(1, len(final)),))]
+        pltpu.SemaphoreType.DMA((n,)), pltpu.SemaphoreType.DMA((n,)), pltpu.SemaphoreType.DMA((2, 2, group)), pltpu.SemaphoreType.DMA((n,)),
+        pltpu.SemaphoreType.DMA((n_par, 8)), pltpu.SemaphoreType.DMA((max(1, len(final)),)), pltpu.SemaphoreType.DMA((d // nw,))]
     cols = n_steps * group * width
     rows = n * tb
     res = pl.pallas_call(
-        functools.partial(mlp_kernel, ts=tuple(ts), steps=steps, n_stacks=len(stacks), first=first, proj=tuple(proj), final=tuple(final), aliased=bool(alias), nw=nw),
+        functools.partial(mlp_kernel, ts=tuple(ts), steps=steps, n_stacks=len(stacks), first=first, proj=tuple(proj), slots=tuple(slot for _, slot in att), final=tuple(final), aliased=bool(alias), nw=nw),
         in_specs=specs, out_specs=[hbm] * len(outs), out_shape=outs, input_output_aliases=alias, scratch_shapes=scratch,
         compiler_params=pltpu.CompilerParams(vmem_limit_bytes=VMEM),
         cost_estimate=pl.CostEstimate(flops=4 * rows * d * cols + 2 * len(proj) * tb * d * d, bytes_accessed=4 * d * cols + 10 * rows * d, transcendentals=rows * cols),
@@ -600,8 +627,8 @@
         y_own = [modulated_norm(tokens[s], shift[s], scale[s]) for s in range(batch)]
         y_full = [gather(y_own[s], tiled=True) for s in range(batch)]
         l_pack = [gather(packs[i]) for i in range(len(chunks))]
+
         w_oa = gather(w_out_attn, tiled=True)
-
         far_ids = jnp.stack([2 * ((xpos + j) % n_x) + cpos for j in range(1, n_x)])
         near_ids = [2 * ((xpos + j) % n_x) + 1 - cpos for j in range(1, n_x)]
         perm = jnp.arange(HEAD)
@@ -617,6 +644,7 @@
         own = (own_pack, lax.dynamic_index_in_dim(bias_n, me, 0))
         mate = (mate_pack, lax.dynamic_index_in_dim(bias_n, me ^ 1, 0))
         left, far, near, qkv, att, spread = {}, {}, {}, {}, {}, {}
+        place = {0: (0, 2), 1: (1, 2), 2: (0, 1)}
         state = {'last': None, 'acc': None, 'out': None}
 
         def turn(x):
@@ -626,11 +654,13 @@
             b0, nb = chunks[i]
             left[i] = (l_pack[i], bias_g[:, b0:b0 + nb])
             state['last'] = pick_call(far_ids, turn(l_pack[i]))
-            far[i] = (cross(state['last']), jnp.stack([bias_n[2 * ((xpos + j) % n_x) + cpos, b0:b0 + nb] for j in range(1, n_x)]))
+            d_pack = cross(state['last'])
+            far[i] = (d_pack, jnp.stack([bias_n[2 * ((xpos + j) % n_x) + cpos, b0:b0 + nb] for j in range(1, n_x)]))
 
         def do_relay(i):
             b0, nb = chunks[i]
-            near[i] = (swap(turn(far[i][0])), jnp.stack([bias_n[j, b0:b0 + nb] for j in near_ids]))
+            e_pack = swap(turn(far[i][0]))
+            near[i] = (e_pack, jnp.stack([bias_n[j, b0:b0 + nb] for j in near_ids]))
 
         def do_qkv(s):
             qkv[s] = qkv_call(turn(y_full[s]), w_all, b_all, gains, hots[s], table, d_local)
@@ -643,9 +673,13 @@
             v_top = top[2 * heads:3 * heads]
             fast = (bound < 100.0) & (v_top * jnp.exp2(bound) < 2.0 ** 110)
             info = jnp.concatenate([(seq - TXT + txt_len[s])[None], fast.astype(jnp.int32)])
-            att[s] = attn_call(info, turn(q), k, v)
+            att[s] = attn_call(info, turn(q), k, v, rows, *place[s], out=att[s - 1] if place[s][0] else None)
             state['last'] = att[s]
-            spread[s] = lax.all_to_all(att[s].reshape(n_tp, rows, d_local), 'tp', 0, 0, tiled=False)
+
+        def do_spread(samples):
+            moved = lax.all_to_all(turn(att[samples[-1]]), 'tp', 0, 0, tiled=False)
+            for s in samples:
+                spread[s] = (moved, place[s][0])
 
         def do_mlp(names, proj=(), final=(), ts=tuple(range(batch))):
             stacks, flat = [], []
@@ -654,8 +688,8 @@
                 for stack in {'O': (own, mate), 'L': (left.get(i),), 'D': (far.get(i), near.get(i))}[name[0]]:
                     stacks.append(stack)
                     n_shards, _, nb = stack[0].shape[:3]
-                    flat += [(len(stacks) - 1, j, b, 2) for j in range(n_shards) for b in range(0, nb, 2)]
-            steps = [flat[i:i + 2] for i in range(0, len(flat), 2)]
+                    flat += [(len(stacks) - 1, j, b, 1) for j in range(n_shards) for b in range(nb)]
+            steps = [flat[i:i + 4] for i in range(0, len(flat), 4)]
             y = [y_own[t] for t in ts]
             acc = state['acc'] and [state['acc'][t] for t in ts]
             if acc:
@@ -678,17 +712,19 @@
         do_attend(0)
         do_relay(0)
         do_send(1)
-        do_mlp(['L1'])
-        do_send(2)
-        do_mlp(['D0', 'L2'])
-        do_relay(1)
+        do_mlp(['L1', 'D0'])
         do_qkv(1)
         do_attend(1)
-        do_mlp(['D1'])
+        do_relay(1)
+        do_send(2)
+        do_mlp(['L2', 'D1'])
         do_qkv(2)
+        do_spread((0, 1))
+        do_attend(2)
         do_relay(2)
-        do_attend(2)
-        do_mlp(['D2'], proj=(0, 1), final=(0, 1))
+        do_mlp(['D2'])
+        do_spread((2,))
+        do_mlp([], proj=(0, 1), final=(0, 1), ts=(0, 1))
         do_mlp([], proj=(2,), final=(2,), ts=(2,))
         return state['out'].reshape(batch, rows, d_model)
 

time: 1020 us -> 986 us (0.967)
  waiting for transfers between devices: 155 us -> 123 us
    ppermute x3, waiting for transfers between devices: 20 us -> 4.79 us  [block_step(): cross = lambda a: lax.ppermute(a, 'dp', twin)]
    all_to_all x3 -> x2, waiting for transfers between devices: 35.9 us -> 22.8 us  [do_spread(): moved = lax.all_to_all(turn(att[samples[-1]]), 'tp', 0, 0, tiled=False)]
    all_gather x7, waiting for transfers between devices: 89.7 us -> 77.2 us  [gather(): return lax.all_gather(a, 'tp', axis=0, tiled=tiled)]
  transfers between devices with their start and end apart: 20 -> 19, of which waited for: 9 -> 10; matrix products, arithmetic and copies ran while one was open for 6% -> 7% of each run, Pallas kernels for 71% -> 73%
where the time goes in v2:
time: 986 us; the launch traced here: 976 us
  Pallas kernels  737 us (75%)
  waiting for transfers between devices  123 us (12%)
  other arithmetic  52.3 us (5%)
  between operations  30.4 us (3%)
  starting transfers between devices  22 us (2%)
  local copies, waits for them, and re-layouts  11.9 us (1%)
    pallas_call x7, Pallas kernels, mlp_call(): pl.pallas_call(functools.partial(mlp_kernel, ts=tuple(ts), steps=steps, n...  371 us
    pallas_call x3, Pallas kernels, attn_call(): pl.pallas_call(functools.partial(attn_kernel, sub=sub, bk=bk), grid_spec=...  180 us
    pallas_call x3, Pallas kernels, qkv_call(): pl.pallas_call(functools.partial(qkv_kernel, sub=sub), grid=(steps,), in_...  127 us
    all_gather x7, waiting for transfers between devices, gather(): return lax.all_gather(a, 'tp', axis=0, tiled=tiled)  77.2 us
    pallas_call x3, Pallas kernels, pick_call(): pl.pallas_call(pick_kernel, grid_spec=pltpu.PrefetchScalarGridSpec(num_sc...  26.5 us
    all_to_all x2, waiting for transfers between devices, do_spread(): moved = lax.all_to_all(turn(att[samples[-1]]), 'tp', 0, 0, tiled=False)  22.8 us
  transfers between devices with their start and end apart: 19, of which 10 were waited for; matrix products, arithmetic and copies ran while one was open for 7% of the time, Pallas kernels for 73%

profile of v2, /device:TPU:112, one launch (start us, length us, event | category | flops | bytes accessed | tf_op | source)
XLA Modules:
  0.0 976.0 jit_solution(6892228518282092321)
XLA Ops:
  6.6 3.4 shard_map.145
  10.8 5.0 shard_map.146
  16.6 5.9 convert_reduce_fusion
  22.5 7.1 fusion.17
  29.7 2.4 collective-permute-start.1
  32.1 3.2 collective-permute-done.1
  35.3 3.6 collective-permute-start.2
  39.0 4.7 collective-permute-done.2
  44.6 9.2 fusion.20
  53.9 9.2 shard_map.147
  63.1 3.6 shard_map.151
  67.5 3.4 shard_map.157
  76.1 1.4 multiply_cosine_fusion.2
  79.8 8.4 shard_map.152.w_ref
  94.7 4.6 fusion.23.hot_ref
  101.8 42.3 %shard_map.148 = (f32[512,3072]{1,0:T(8,128)}, f32[512,3072]{1,0:T(8,128)}, f32[512,3072]{1,0:T(8,128)}) custom-call(bf16[512,3072]{1,0:T(8,128)(2,1)} %get-tuple-element.111.refs_0_, bf16[512,3072]{1,0:T(8,128)(2,1)} %get-tuple-element.110.refs_1_, bf16[512,3072]{1,0:T(8,128)(2,1)} %get-tuple-element.109.refs_2_, bf16[1,2,6,128,3072]{4,3,2,1,0:T(8,128)(2,1)} %bitcast.116, ...), custom_call_target="tpu_custom_call" | custom-call | flops 28991029248 | bytes 66060288 | tf_op jit(solution)/shard_map/pallas_call | solution.py:429
  144.1 9.4 shard_map.149
  153.5 2.0 collective-permute-start.4
  155.6 55.2 %shard_map.150 = (f32[512,3072]{1,0:T(8,128)}, f32[512,3072]{1,0:T(8,128)}, f32[512,3072]{1,0:T(8,128)}) custom-call(bf16[512,3072]{1,0:T(8,128)(2,1)} %get-tuple-element.111.refs_0_, bf16[512,3072]{1,0:T(8,128)(2,1)} %get-tuple-element.110.refs_1_, bf16[512,3072]{1,0:T(8,128)(2,1)} %get-tuple-element.109.refs_2_, f32[512,3072]{1,0:T(8,128)} %get-tuple-element.56.refs_3_, ...), custom_call_target="tpu_custom_call" | custom-call | flops 38654705664 | bytes 72351744 | tf_op jit(solution)/shard_map/pallas_call | solution.py:429
  210.8 39.7 %all-gather.11.cloned.1.call-done.y_ref = bf16[4096,3072]{1,0:T(8,128)(2,1)} async-done(((bf16[512,3072]{1,0:T(8,128)(2,1)}), bf16[4096,3072]{1,0:T(8,128)(2,1)}) %all-gather.11.cloned.1.call-update) | async-done | bytes 25165840 | tf_op jit(solution)/shard_map/all_gather | solution.py:597
  250.4 42.2 %shard_map.153 = (bf16[4096,384]{1,0:T(8,128)(2,1)}, bf16[4096,384]{1,0:T(8,128)(2,1)}, bf16[4096,384]{1,0:T(8,128)(2,1)}, f32[8,16,128]{2,1,0:T(8,128)}) custom-call(bf16[4096,3072]{1,0:T(8,128)(2,1)} %all-gather.11.cloned.1.call-done.y_ref, bf16[3072,1280]{1,0:T(8,128)(2,1)} %shard_map.152.w_ref, f32[1,1280]{1,0:T(1,128)} %broadcast_in_dim.43.b_ref, ...), custom_call_target="tpu_custom_call" | custom-call | flops 32212254720 | bytes 35651584 | tf_op jit(solution)/shard_map/pallas_call | solution.py:65
  294.3 60.1 %shard_map.154.refs_0_ = bf16[8,2,512,384]{3,2,1,0:T(8,128)(2,1)} custom-call(s32[4]{0:T(128)} %pad_add_fusion.1.info_ref, bf16[4096,384]{1,0:T(8,128)(2,1)} %get-tuple-element.63.q_ref, bf16[4096,384]{1,0:T(8,128)(2,1)} %get-tuple-element.64.k_ref, bf16[4096,384]{1,0:T(8,128)(2,1)} %get-tuple-element.65.v_ref), custom_call_target="tpu_custom_call" | custom-call | flops 51539607552 | bytes 12582912 | tf_op jit(solution)/shard_map/pallas_call | solution.py:156
  354.5 4.8 collective-permute-done.4.refs_7_
  366.1 4.7 fusion.26.hot_ref
  371.4 1.7 constant_dynamic-slice_fusion.4
  373.7 9.0 shard_map.155
  382.7 1.5 collective-permute-start.6
  384.2 88.1 %shard_map.156 = (f32[512,3072]{1,0:T(8,128)}, f32[512,3072]{1,0:T(8,128)}, f32[512,3072]{1,0:T(8,128)}) custom-call(bf16[512,3072]{1,0:T(8,128)(2,1)} %get-tuple-element.111.refs_0_, bf16[512,3072]{1,0:T(8,128)(2,1)} %get-tuple-element.110.refs_1_, bf16[512,3072]{1,0:T(8,128)(2,1)} %get-tuple-element.109.refs_2_, f32[512,3072]{1,0:T(8,128)} %get-tuple-element.67.refs_3_, ...), custom_call_target="tpu_custom_call" | custom-call | flops 67645734912 | bytes 91226112 | tf_op jit(solution)/shard_map/pallas_call | solution.py:429
  472.3 16.0 %all-gather.13.cloned.1.call-done.y_ref = bf16[4096,3072]{1,0:T(8,128)(2,1)} async-done(((bf16[512,3072]{1,0:T(8,128)(2,1)}), bf16[4096,3072]{1,0:T(8,128)(2,1)}) %all-gather.13.cloned.1.call-update) | async-done | bytes 25165840 | tf_op jit(solution)/shard_map/all_gather | solution.py:597
  488.2 42.2 %shard_map.158 = (bf16[4096,384]{1,0:T(8,128)(2,1)}, bf16[4096,384]{1,0:T(8,128)(2,1)}, bf16[4096,384]{1,0:T(8,128)(2,1)}, f32[8,16,128]{2,1,0:T(8,128)}) custom-call(bf16[4096,3072]{1,0:T(8,128)(2,1)} %all-gather.13.cloned.1.call-done.y_ref, bf16[3072,1280]{1,0:T(8,128)(2,1)} %shard_map.152.w_ref, f32[1,1280]{1,0:T(1,128)} %broadcast_in_dim.43.b_ref, ...), custom_call_target="tpu_custom_call" | custom-call | flops 32212254720 | bytes 35651584 | tf_op jit(solution)/shard_map/pallas_call | solution.py:65
  532.2 59.8 %shard_map.159 = bf16[8,2,512,384]{3,2,1,0:T(8,128)(2,1)} custom-call(s32[4]{0:T(128)} %pad_add_fusion.2.info_ref, bf16[4096,384]{1,0:T(8,128)(2,1)} %get-tuple-element.75.q_ref, bf16[4096,384]{1,0:T(8,128)(2,1)} %get-tuple-element.76.k_ref, bf16[4096,384]{1,0:T(8,128)(2,1)} %get-tuple-element.77.v_ref, ...), custom_call_target="tpu_custom_call", output_to_operand_aliasing={{}: (4, {})} | custom-call | flops 51539607552 | bytes 12582912 | tf_op jit(solution)/shard_map/pallas_call | solution.py:156
  598.7 4.7 fusion.29.hot_ref
  604.6 3.2 all-gather.23.cloned.1.call-done
  607.8 8.1 shard_map.160
  615.9 1.4 collective-permute-start.8
  617.3 90.0 %shard_map.161 = (f32[512,3072]{1,0:T(8,128)}, f32[512,3072]{1,0:T(8,128)}, f32[512,3072]{1,0:T(8,128)}) custom-call(bf16[512,3072]{1,0:T(8,128)(2,1)} %get-tuple-element.111.refs_0_, bf16[512,3072]{1,0:T(8,128)(2,1)} %get-tuple-element.110.refs_1_, bf16[512,3072]{1,0:T(8,128)(2,1)} %get-tuple-element.109.refs_2_, f32[512,3072]{1,0:T(8,128)} %get-tuple-element.79.refs_3_, ...), custom_call_target="tpu_custom_call" | custom-call | flops 67645734912 | bytes 91226112 | tf_op jit(solution)/shard_map/pallas_call | solution.py:429
  707.4 18.4 %all-gather.15.cloned.1.call-done.y_ref = bf16[4096,3072]{1,0:T(8,128)(2,1)} async-done(((bf16[512,3072]{1,0:T(8,128)(2,1)}), bf16[4096,3072]{1,0:T(8,128)(2,1)}) %all-gather.15.cloned.1.call-update) | async-done | bytes 25165840 | tf_op jit(solution)/shard_map/all_gather | solution.py:597
  725.8 42.1 %shard_map.162 = (bf16[4096,384]{1,0:T(8,128)(2,1)}, bf16[4096,384]{1,0:T(8,128)(2,1)}, bf16[4096,384]{1,0:T(8,128)(2,1)}, f32[8,16,128]{2,1,0:T(8,128)}) custom-call(bf16[4096,3072]{1,0:T(8,128)(2,1)} %all-gather.15.cloned.1.call-done.y_ref, bf16[3072,1280]{1,0:T(8,128)(2,1)} %shard_map.152.w_ref, f32[1,1280]{1,0:T(1,128)} %broadcast_in_dim.43.b_ref, ...), custom_call_target="tpu_custom_call" | custom-call | flops 32212254720 | bytes 35651584 | tf_op jit(solution)/shard_map/pallas_call | solution.py:65
  769.7 59.6 %shard_map.163 = bf16[8,1,512,384]{3,2,1,0:T(8,128)(2,1)} custom-call(s32[4]{0:T(128)} %pad_add_fusion.3.info_ref, bf16[4096,384]{1,0:T(8,128)(2,1)} %get-tuple-element.87.q_ref, bf16[4096,384]{1,0:T(8,128)(2,1)} %get-tuple-element.88.k_ref, bf16[4096,384]{1,0:T(8,128)(2,1)} %get-tuple-element.89.v_ref), custom_call_target="tpu_custom_call" | custom-call | flops 51539607552 | bytes 12582912 | tf_op jit(solution)/shard_map/pallas_call | solution.py:156
  829.6 5.1 all-to-all-start
  835.4 8.9 collective-permute-done.9.refs_7_
  844.3 43.2 %shard_map.164 = (f32[512,3072]{1,0:T(8,128)}, f32[512,3072]{1,0:T(8,128)}, f32[512,3072]{1,0:T(8,128)}) custom-call(bf16[512,3072]{1,0:T(8,128)(2,1)} %get-tuple-element.111.refs_0_, bf16[512,3072]{1,0:T(8,128)(2,1)} %get-tuple-element.110.refs_1_, bf16[512,3072]{1,0:T(8,128)(2,1)} %get-tuple-element.109.refs_2_, f32[512,3072]{1,0:T(8,128)} %get-tuple-element.90.refs_3_, ...), custom_call_target="tpu_custom_call" | custom-call | flops 28991029248 | bytes 66060288 | tf_op jit(solution)/shard_map/pallas_call | solution.py:429
  887.6 19.2 %all-to-all-done.refs_2_.refs_3_ = bf16[8,2,512,384]{3,2,1,0:T(8,128)(2,1)} async-done(((bf16[8,2,512,384]{3,2,1,0:T(8,128)(2,1)}), bf16[8,2,512,384]{3,2,1,0:T(8,128)(2,1)}, u32[]{:S(2)}, u32[]{:S(2)}) %all-to-all-start) | async-done | bytes 6291488 | tf_op jit(solution)/shard_map/all_to_all | solution.py:680
  906.8 4.6 all-to-all-start.1
  911.4 1.4 slice.171.refs_6_.refs_4_
  912.8 33.2 %shard_map.165.refs_6_ = bf16[1536,3072]{1,0:T(8,128)(2,1)} custom-call(f32[512,3072]{1,0:T(8,128)} %get-tuple-element.96.refs_0_, f32[512,3072]{1,0:T(8,128)} %get-tuple-element.97.refs_1_, bf16[8,2,512,384]{3,2,1,0:T(8,128)(2,1)} %all-to-all-done.refs_2_.refs_3_, bf16[8,2,512,384]{3,2,1,0:T(8,128)(2,1)} %all-to-all-done.refs_2_.refs_3_, ...), custom_call_target="tpu_custom_call" | custom-call | flops 19327352832 | bytes 31457280 | tf_op jit(solution)/shard_map/pallas_call | solution.py:429
  946.1 3.6 all-to-all-done.1.refs_1_
  949.7 19.1 %shard_map.166 = bf16[1536,3072]{1,0:T(8,128)(2,1)} custom-call(f32[512,3072]{1,0:T(8,128)} %get-tuple-element.99.refs_0_, bf16[8,1,512,384]{3,2,1,0:T(8,128)(2,1)} %all-to-all-done.1.refs_1_, bf16[3,2,4,128,3072]{4,3,2,1,0:T(8,128)(2,1)} %bitcast.114, bf16[1536,3072]{1,0:T(8,128)(2,1)} %bitcast.106, ...), custom_call_target="tpu_custom_call", output_to_operand_aliasing={{}: (6, {})} | custom-call | flops 9663676416 | bytes 15728640 | tf_op jit(solution)/shard_map/pallas_call | solution.py:429
  (155 shorter events, 25.8 us)
Async XLA Ops:
  6.5 137.6 %all-gather.19.cloned.1.call-start = ((), (), s32[]{:S(2)}) async-start(), calls=%async_computation.6 | async-start | bytes 28311552 | tf_op jit(solution)/shard_map/all_gather | solution.py:597
  6.6 3.6 copy-start.2
  10.0 240.4 %all-gather.11.cloned.1.call-start = ((), (), s32[]{:S(2)}) async-start(), calls=%async_computation.2 | async-start | bytes 28311552 | tf_op jit(solution)/shard_map/all_gather | solution.py:597
  10.8 5.7 copy-start.8
  16.5 13.1 %collective-permute-start = (f32[1,4992]{1,0:T(1,128)S(1)}, f32[1,4992]{1,0:T(1,128)S(1)}, u32[]{:S(2)}, u32[]{:S(2)}) collective-permute-start(f32[1,4992]{1,0:T(1,128)S(1)} %broadcast_in_dim.38), channel_id=1, source_target_pairs={{0,1},{1,0},{2,3},{3,2},{4,5},{5,4},{6,7},{7,6},{8,9},{9,8},{10,11... | collective-permute-start | bytes 59912 | tf_op jit(solution)/shard_map/ppermute | solution.py:602
  22.5 21.3 %copy-start.3 = (f32[9216]{0:T(1024)S(1)}, f32[9216]{0:T(1024)}, u32[]{:S(2)}) copy-start(f32[9216]{0:T(1024)} %param.20) | copy-start | bytes 110596
  29.7 5.6 collective-permute-start.1
  35.3 8.3 collective-permute-start.2
  43.8 0.7 copy-start
  53.8 319.9 %all-gather.21.cloned.1.call-start = ((), (), s32[]{:S(2)}) async-start(), calls=%async_computation.7 | async-start | bytes 28311552 | tf_op jit(solution)/shard_map/all_gather | solution.py:597
  66.7 421.5 %all-gather.13.cloned.1.call-start = ((), (), s32[]{:S(2)}) async-start(), calls=%async_computation.3 | async-start | bytes 28311552 | tf_op jit(solution)/shard_map/all_gather | solution.py:597
  67.4 540.4 %all-gather.23.cloned.1.call-start = ((), (), s32[]{:S(2)}) async-start(), calls=%async_computation.8 | async-start | bytes 28311552 | tf_op jit(solution)/shard_map/all_gather | solution.py:597
  67.4 4.1 copy-start.7
  67.5 6.1 slice-start
  67.5 6.5 copy-start.22
  67.5 6.7 copy-start.23
  67.5 7.6 copy-start.9
  67.5 8.3 copy-start.6
  71.0 654.8 %all-gather.15.cloned.1.call-start = ((), (), s32[]{:S(2)}) async-start(), calls=%async_computation.4 | async-start | bytes 28311552 | tf_op jit(solution)/shard_map/all_gather | solution.py:597
  71.1 30.7 %collective-permute-start.3 = (bf16[1,2,6,128,3072]{4,3,2,1,0:T(8,128)(2,1)}, bf16[1,2,6,128,3072]{4,3,2,1,0:T(8,128)(2,1)}, u32[]{:S(2)}, u32[]{:S(2)}) collective-permute-start(bf16[1,2,6,128,3072]{4,3,2,1,0:T(8,128)(2,1)} %bitcast.115), channel_id=1, source_target_pairs={{0,1},{1,0},{2,3},{3,2},{4,5},{5,4},{6,7},{7,6},{8,9},{9,8},{10,11... | collective-permute-start | bytes 28311560 | tf_op jit(solution)/shard_map/ppermute | solution.py:607
  79.5 833.3 %all-gather.17.cloned.1.call-start = ((), (), s32[]{:S(2)}) async-start(), calls=%async_computation.5 | async-start | bytes 21233664 | tf_op jit(solution)/shard_map/all_gather | solution.py:597
  99.4 1.2 copy-start.1
  153.5 205.7 %collective-permute-start.4 = (bf16[3,2,2,128,3072]{4,3,2,1,0:T(8,128)(2,1)}, bf16[3,2,2,128,3072]{4,3,2,1,0:T(8,128)(2,1)}, u32[]{:S(2)}, u32[]{:S(2)}) collective-permute-start(bf16[3,2,2,128,3072]{4,3,2,1,0:T(8,128)(2,1)} %shard_map.149), channel_id=1, source_target_pairs={{0,8},{8,0},{1,9},{9,1},{2,10},{10,2},{3,11},{11,3},{4,12},{12,4},... | collective-permute-start | bytes 28311560 | tf_op jit(solution)/shard_map/ppermute | solution.py:608
  294.3 76.5 %copy-start.5 = (f32[8,2,128]{2,0,1:T(8,128)S(1)}, f32[8,2,128]{2,0,1:T(8,128)}, u32[]{:S(2)}) copy-start(f32[8,2,128]{2,0,1:T(8,128)} %get-tuple-element.139) | copy-start | bytes 24580
  359.3 24.9 %collective-permute-start.5 = (bf16[3,2,2,128,3072]{4,3,2,1,0:T(8,128)(2,1)}, bf16[3,2,2,128,3072]{4,3,2,1,0:T(8,128)(2,1)}, u32[]{:S(2)}, u32[]{:S(2)}) collective-permute-start(bf16[3,2,2,128,3072]{4,3,2,1,0:T(8,128)(2,1)} %collective-permute-done.4.refs_7_), channel_id=1, source_target_pairs={{0,1},{1,0},{2,3},{3,2},{4,5},{5,4},{6,7},{7,6},{8,9},{9,8},{10,11... | collective-permute-start | bytes 28311560 | tf_op jit(solution)/shard_map/ppermute | solution.py:607
  382.7 209.3 %collective-permute-start.6 = (bf16[3,2,2,128,3072]{4,3,2,1,0:T(8,128)(2,1)}, bf16[3,2,2,128,3072]{4,3,2,1,0:T(8,128)(2,1)}, u32[]{:S(2)}, u32[]{:S(2)}) collective-permute-start(bf16[3,2,2,128,3072]{4,3,2,1,0:T(8,128)(2,1)} %shard_map.155), channel_id=1, source_target_pairs={{0,8},{8,0},{1,9},{9,1},{2,10},{10,2},{3,11},{11,3},{4,12},{12,4},... | collective-permute-start | bytes 28311560 | tf_op jit(solution)/shard_map/ppermute | solution.py:608
  532.1 71.3 %copy-start.4 = (f32[8,2,128]{2,0,1:T(8,128)S(1)}, f32[8,2,128]{2,0,1:T(8,128)}, u32[]{:S(2)}) copy-start(f32[8,2,128]{2,0,1:T(8,128)} %get-tuple-element.138) | copy-start | bytes 24580
  532.1 71.9 %copy-start.16 = (f32[1,2,128]{2,0,1:T(1,128)S(1)}, f32[1,2,128]{2,0,1:T(1,128)}, u32[]{:S(2)}) copy-start(f32[1,2,128]{2,0,1:T(1,128)} %get-tuple-element.125) | copy-start | bytes 3076
  532.1 71.9 %copy-start.17 = (f32[1,2,128]{2,0,1:T(1,128)S(1)}, f32[1,2,128]{2,0,1:T(1,128)}, u32[]{:S(2)}) copy-start(f32[1,2,128]{2,0,1:T(1,128)} %get-tuple-element.126) | copy-start | bytes 3076
  532.1 71.9 %copy-start.18 = (f32[1,2,128]{2,0,1:T(1,128)S(1)}, f32[1,2,128]{2,0,1:T(1,128)}, u32[]{:S(2)}) copy-start(f32[1,2,128]{2,0,1:T(1,128)} %get-tuple-element.127) | copy-start | bytes 3076
  532.1 71.9 %copy-start.19 = (f32[1,2,128]{2,0,1:T(1,128)S(1)}, f32[1,2,128]{2,0,1:T(1,128)}, u32[]{:S(2)}) copy-start(f32[1,2,128]{2,0,1:T(1,128)} %get-tuple-element.128) | copy-start | bytes 3076
  532.2 71.8 %copy-start.20 = (f32[1,2,128]{2,0,1:T(1,128)S(1)}, f32[1,2,128]{2,0,1:T(1,128)}, u32[]{:S(2)}) copy-start(f32[1,2,128]{2,0,1:T(1,128)} %get-tuple-element.129) | copy-start | bytes 3076
  532.2 71.8 %copy-start.21 = (f32[1,2,128]{2,0,1:T(1,128)S(1)}, f32[1,2,128]{2,0,1:T(1,128)}, u32[]{:S(2)}) copy-start(f32[1,2,128]{2,0,1:T(1,128)} %get-tuple-element.130) | copy-start | bytes 3076
  592.0 25.4 %collective-permute-start.7 = (bf16[3,2,2,128,3072]{4,3,2,1,0:T(8,128)(2,1)}, bf16[3,2,2,128,3072]{4,3,2,1,0:T(8,128)(2,1)}, u32[]{:S(2)}, u32[]{:S(2)}) collective-permute-start(bf16[3,2,2,128,3072]{4,3,2,1,0:T(8,128)(2,1)} %collective-permute-done.6.refs_7_), channel_id=1, source_target_pairs={{0,1},{1,0},{2,3},{3,2},{4,5},{5,4},{6,7},{7,6},{8,9},{9,8},{10,11... | collective-permute-start | bytes 28311560 | tf_op jit(solution)/shard_map/ppermute | solution.py:607
  615.9 213.4 %collective-permute-start.8 = (bf16[3,2,2,128,3072]{4,3,2,1,0:T(8,128)(2,1)}, bf16[3,2,2,128,3072]{4,3,2,1,0:T(8,128)(2,1)}, u32[]{:S(2)}, u32[]{:S(2)}) collective-permute-start(bf16[3,2,2,128,3072]{4,3,2,1,0:T(8,128)(2,1)} %shard_map.160), channel_id=1, source_target_pairs={{0,8},{8,0},{1,9},{9,1},{2,10},{10,2},{3,11},{11,3},{4,12},{12,4},... | collective-permute-start | bytes 28311560 | tf_op jit(solution)/shard_map/ppermute | solution.py:608
  829.2 5.5 copy-start.10
  829.2 5.5 copy-start.11
  829.2 5.6 copy-start.12
  829.2 5.6 copy-start.13
  829.2 5.6 copy-start.14
  829.2 5.6 copy-start.15
  829.3 15.1 %collective-permute-start.9 = (bf16[3,2,2,128,3072]{4,3,2,1,0:T(8,128)(2,1)}, bf16[3,2,2,128,3072]{4,3,2,1,0:T(8,128)(2,1)}, u32[]{:S(2)}, u32[]{:S(2)}) collective-permute-start(bf16[3,2,2,128,3072]{4,3,2,1,0:T(8,128)(2,1)} %collective-permute-done.8.refs_6_), channel_id=1, source_target_pairs={{0,1},{1,0},{2,3},{3,2},{4,5},{5,4},{6,7},{7,6},{8,9},{9,8},{10,11... | collective-permute-start | bytes 28311560 | tf_op jit(solution)/shard_map/ppermute | solution.py:607
  829.6 77.2 %all-to-all-start = ((bf16[8,2,512,384]{3,2,1,0:T(8,128)(2,1)}), bf16[8,2,512,384]{3,2,1,0:T(8,128)(2,1)}, u32[]{:S(2)}, u32[]{:S(2)}) async-start(bf16[8,2,512,384]{3,2,1,0:T(8,128)(2,1)} %shard_map.159), calls=%async_computation | async-start | bytes 12582912 | tf_op jit(solution)/shard_map/all_to_all | solution.py:680
  906.8 42.9 %all-to-all-start.1 = ((bf16[8,1,512,384]{3,2,1,0:T(8,128)(2,1)}), bf16[8,1,512,384]{3,2,1,0:T(8,128)(2,1)}, u32[]{:S(2)}, u32[]{:S(2)}) async-start(bf16[8,1,512,384]{3,2,1,0:T(8,128)(2,1)} %shard_map.163), calls=%async_computation.1 | async-start | bytes 6291456 | tf_op jit(solution)/shard_map/all_to_all | solution.py:680
Sparse Core Ops, SparseCore 0:
  10.1 121.5 all-gather.18
  133.3 117.0 all-gather.10
  252.0 118.1 all-gather.20
  371.6 116.5 all-gather.12
  489.6 118.1 all-gather.22
  609.2 116.5 all-gather.14
  727.4 90.5 all-gather.16
